TPU v7x, 128 devices: a whole 4x4x4 slice. The times are simulated.
128 devices in a mesh: gz: 128 (over y, z, x, core).
Axes of the slice: x: 4, y: 4, z: 4, core: 2. Of those that a mesh axis runs over, the one named last changes fastest.
Arguments:
- marker_positions: float32 [16384, 3, 256], P('gz'), may hold values from 0 to 1
- marker_forces: float32 [16384, 3, 256], P('gz'), may hold values from -48 to 48
- dest_slab: int32 [16384, 1], P('gz'), may hold values from 0 to 127; in each aligned block of 128 rows (0 to 127, 128 to 255, ...) at most 2 rows name the same one
- base_cells: int32 [16384, 2], P('gz'), may hold values from 0 to 127
- fluid_source: float32 [512, 3, 128, 128], P('gz'), may hold values from -7 to 7
Outputs:
- velocity: float32 [512, 3, 128, 128], P('gz')
- marker_velocity: float32 [16384, 3, 256], P('gz')
Inputs may be any that keep to these rules, and one draw needn't show every extreme that they name: `dest_slab`: among the blocks of one device no slab is named more than 2 times.
All inputs are finite; a program needn't handle non-finite values.
Results may differ from a plain program's by a relative error of at most 0.00096.
Values may be sent and summed in bfloat16 or wider, within the bound.
No kernel may reach another device: no remote copies, remote signals or barrier semaphores. Data moves between devices by JAX's collectives and lax.ppermute only.
A program may use at most 256 MiB of HBM per device.

v0:
```python
import math

import jax
import jax.numpy as jnp
from jax import lax
from jax.experimental import pallas as pl
from jax.experimental.pallas import tpu as pltpu
from jax.sharding import Mesh
from jax.sharding import PartitionSpec as P

AX = ("hi", "lo")
LOCAL = 8
BOX = 16
CZ = 4
HALF = CZ * BOX
ROWS = 3 * BOX
SCREEN = 1.0 / 64.0
RELAX = 2.0 / 3.0
INTERPRET = False
F32 = jnp.float32
BF16 = jnp.bfloat16
HIGH = lax.Precision.HIGHEST


def level(index):
    q = 0.25**index
    return q, SCREEN + 6.0 * q, RELAX / (SCREEN + 6.0 * q)


def call(body, out_shape, in_specs=None, scratch=(), megabytes=24):
    options = {} if in_specs is None else {"in_specs": in_specs}
    return pl.pallas_call(
        body,
        out_shape=out_shape,
        scratch_shapes=list(scratch),
        interpret=INTERPRET,
        compiler_params=pltpu.CompilerParams(vmem_limit_bytes=megabytes << 20),
        **options,
    )


def shaped(shape, dtype, near=True):
    if near and not INTERPRET:
        return pltpu.VMEM(shape, dtype)
    return jax.ShapeDtypeStruct(shape, dtype)


def near(value):
    return value if INTERPRET else pltpu.with_memory_space_constraint(value, pltpu.VMEM)


VMEM = pl.BlockSpec(memory_space=pltpu.VMEM)
SMEM = pl.BlockSpec(memory_space=pltpu.SMEM)


def far(value):
    return value if INTERPRET else pltpu.with_memory_space_constraint(value, pltpu.HBM)


def iota(shape, dim):
    return lax.broadcasted_iota(jnp.int32, shape, dim)


COS = (
    0.13884009367929634,
    0.008677498753340366,
    0.0001925760632832398,
    2.2059131886721028e-06,
    1.644977822379996e-08,
)


def phi(offset):
    inside = jnp.maximum(4.0 - offset * offset, 0.0)
    value = inside * COS[-1] + COS[-2]
    for coefficient in COS[-3::-1]:
        value = value * inside + coefficient
    value = value * inside
    return value * value


def split(value):
    high = value.astype(BF16)
    return high, (value - high.astype(F32)).astype(BF16)


def box_weights(pos_ref, block):
    cells = iota((BOX, 256), 0).astype(F32)
    levels = iota((8, 256), 0).astype(F32)
    row = pl.ds(block, 1)
    along_x = 2.0 + (BOX - 5) * pos_ref[0, row, :]
    along_y = 2.0 + (BOX - 5) * pos_ref[1, row, :]
    height = (CZ - 1) * pos_ref[2, row, :]
    return phi(along_x - cells), phi(along_y - cells), phi(height - levels)


def by_levels(weight_y, weight_z):
    return split(jnp.concatenate([weight_z[k : k + 1] * weight_y for k in range(CZ)], axis=0))


PIECES = (2 * BOX, 3 * BOX, 3 * BOX - 1)


def together(count, most):
    return math.gcd(count, most)


def build_kernel(
    dest_ref, base_ref, pos_ref, frc_ref, fluid_ref, out_ref, stage_ref, count_ref
):
    slots = out_ref.shape[0]
    blocks = pos_ref.shape[1]
    group = together(blocks, 16)

    def clear(t, carry):
        count_ref[t] = 0
        stage_ref[t, 0:8, :] = jnp.zeros((8, 128), F32)
        return carry

    lax.fori_loop(0, slots, clear, 0, unroll=4)
    lane = iota((8, 128), 1)
    top = iota((8, 128), 0) == 0

    def one(block):
        weight_x, weight_y, weight_z = box_weights(pos_ref, block)
        loaded = [frc_ref[c, pl.ds(block, 1), :] * weight_x for c in range(3)]
        high, low = split(jnp.concatenate(loaded, axis=0))
        right = jnp.concatenate(by_levels(weight_y, weight_z), axis=0)
        dims = (((1,), (1,)), ((), ()))
        box = lax.dot_general(high, right, dims, preferred_element_type=F32)
        box = box + lax.dot_general(low, right, dims, preferred_element_type=F32)
        box = box + pltpu.roll(box, HALF, 1)
        base_x = base_ref[0, block].astype(F32) + 1.0
        base_y = base_ref[1, block].astype(F32)
        tiles = [box[8 * n : 8 * n + 8] for n in range(6)]
        rounded = [tile.astype(BF16).astype(F32) for tile in tiles]
        sums = [rounded[2 * c] + rounded[2 * c + 1] for c in range(3)]
        tiles[0] = jnp.where(top & (lane % HALF == 0), base_x, tiles[0])
        tiles[0] = jnp.where(top & (lane % HALF == BOX), base_y, tiles[0])
        return tiles, sums

    def several(step, carry):
        results = []
        for n in range(group):
            tiles, sums = one(step * group + n)
            results.append(tiles)
            carry = tuple(a + b for a, b in zip(carry, sums))
        for n in range(group):
            target = dest_ref[0, step * group + n]
            order = count_ref[target]
            count_ref[target] = order + 1
            mine = lane // HALF == order
            for m in range(6):
                rows = slice(8 * m, 8 * m + 8)
                stage_ref[target, rows, :] = jnp.where(
                    mine, results[n][m], stage_ref[target, rows, :]
                )
        return carry

    fluid = []
    for c in range(3):
        column = fluid_ref[0, c] + fluid_ref[1, c] + (fluid_ref[2, c] + fluid_ref[3, c])
        fluid.append(jnp.sum(column.reshape(16, 8, 128), axis=0))
    zero = jnp.zeros((8, 128), F32)
    boxes = lax.fori_loop(0, blocks // group, several, (zero, zero, zero))
    fluid = [a + 0.5 * b for a, b in zip(fluid, boxes)]
    pieces = []
    for c in range(3):
        rest = jnp.broadcast_to(jnp.sum(fluid[c], axis=(0, 1), keepdims=True), (8, 128))
        marked = jnp.zeros((8, 128), F32)
        for place_of in PIECES:
            part = rest.astype(BF16).astype(F32)
            marked = jnp.where(lane == place_of, part, marked)
            rest = rest - part
        pieces.append(marked)
    held = top & ((lane == PIECES[0]) | (lane == PIECES[1]) | (lane == PIECES[2]))

    def finish(t, carry):
        tiles = []
        for c in range(3):
            row = BOX * c
            tiles.append(jnp.where(held, pieces[c], stage_ref[t, row : row + 8, :]))
            tiles.append(stage_ref[t, row + 8 : row + BOX, :])
        out_ref[t] = jnp.concatenate(tiles, axis=0).astype(BF16)
        return carry

    lax.fori_loop(0, slots, finish, 0, unroll=4)


def build(dest, base, positions, forces, fluid, slots):
    return call(
        build_kernel,
        shaped((slots, ROWS, 128), BF16),
        [SMEM, SMEM, VMEM, VMEM, VMEM],
        [pltpu.VMEM((slots, ROWS, 128), F32), pltpu.SMEM((slots,), jnp.int32)],
    )(*map(far, (dest, base, positions, forces, fluid)))


def flat_ring(x):
    rows = x.shape[-2]
    ax = x.ndim - 2
    return (
        pltpu.roll(x, 1, ax)
        + pltpu.roll(x, rows - 1, ax)
        + (pltpu.roll(x, 1, ax + 1) + pltpu.roll(x, 127, ax + 1))
    )


def group_ring(x):
    rows = x.shape[-2]
    ax = x.ndim - 2
    lane = iota(x.shape, ax + 1) & 31
    before = jnp.where(lane == 0, pltpu.roll(x, 97, ax + 1), pltpu.roll(x, 1, ax + 1))
    after = jnp.where(lane == 31, pltpu.roll(x, 31, ax + 1), pltpu.roll(x, 127, ax + 1))
    return pltpu.roll(x, 1, ax) + pltpu.roll(x, rows - 1, ax) + (before + after)


def start_of(b, below, above, ring, index):
    q, _, w = level(index)
    return w * ((4.0 / 3.0) * b + (w * q) * (ring(b) + (below + above)))


def left_of(b, u, below, above, ring, index):
    q, diag, _ = level(index)
    return b - diag * u + q * (ring(u) + (below + above))


def sweep_of(b, u, below, above, ring, index):
    q, _, w = level(index)
    return (1.0 - RELAX) * u + (w * b + (w * q) * (ring(u) + (below + above)))


def dot(left, right):
    return lax.dot_general(
        left, right, (((1,), (0,)), ((), ())), precision=HIGH, preferred_element_type=F32
    )


def lanes(test):
    return test(iota((128, 128), 0), iota((128, 128), 1))


def place_kernel(
    meta_ref, pay_ref, fluid_ref,
    src_ref, up_ref, down_ref, up2_ref, down2_ref, lift_ref,
    grid_ref, u_ref, sum_ref,
):
    slots = pay_ref.shape[0]
    lane = iota((8, 128), 1)
    sub = iota((8, 128), 0)
    for z in range(CZ):
        for c in range(3):
            grid_ref[3 * z + c, 0:128, :] = fluid_ref[z, c]
            grid_ref[3 * z + c, 128:144, :] = jnp.zeros((16, 128), F32)

    def turned(tile, order, head, base_y):
        base_x = jnp.maximum(head - 1, 0)
        shift = base_x & 7
        row = pl.multiple_of(base_x - shift, 8)
        window = (lane - base_y) & 127
        inside = (window >= 1) & (window <= BOX - 2) & (head > 0)
        late = inside & (sub >= shift)
        early = inside & (sub < shift)
        pieces = [pltpu.roll(tile[8 * n : 8 * n + 8], shift, 0) for n in range(6)]
        values = []
        for k in range(CZ):
            step = (base_y - HALF * order - BOX * k) & 127
            values.append([pltpu.roll(piece, step, 1) for piece in pieces])
        return row, late, early, values

    def add(row, late, early, values):
        for k in range(CZ):
            for c in range(3):
                first, second = values[k][2 * c], values[k][2 * c + 1]
                kc = 3 * k + c
                grid_ref[kc, pl.ds(row, 8), :] += jnp.where(late, first, 0.0)
                grid_ref[kc, pl.ds(row + 8, 8), :] += jnp.where(
                    early, first, jnp.where(late, second, 0.0)
                )
                grid_ref[kc, pl.ds(row + 16, 8), :] += jnp.where(early, second, 0.0)

    group = together(slots, 8)

    def several(step, carry):
        found = []
        for n in range(group):
            d = step * group + n
            tile = pay_ref[d].astype(F32)
            carry = tuple(
                carry[c] + jnp.where(held, tile[BOX * c : BOX * c + 8], 0.0) for c in range(3)
            )
            for order in range(2):
                at = 8 * d + 4 * order
                found.append(turned(tile, order, meta_ref[at], meta_ref[at + 1]))
        for one in found:
            add(*one)
        return carry

    held = (sub == 0) & ((lane == PIECES[0]) | (lane == PIECES[1]) | (lane == PIECES[2]))
    zero = jnp.zeros((8, 128), F32)
    totals = lax.fori_loop(0, slots // group, several, (zero, zero, zero))
    factor = (1.0 - level(3)[2] * SCREEN) ** 6 / SCREEN
    for index in range(3):
        factor = factor * (1.0 - level(index)[2] * SCREEN) ** 2
    scale = factor / (slots * CZ * 128.0 * 128.0)
    lift_ref[...] = zero
    for c in range(3):
        total = jnp.sum(totals[c], axis=(0, 1), keepdims=True)
        lift_ref[c : c + 1, :] = jnp.broadcast_to(total * scale, (1, 128))
    pool = [
        jnp.where(lanes(lambda r, l: (r // 2 == (l & 63)) & (l // 64 == half)), 0.125, 0.0)
        for half in range(2)
    ]
    q, _, w = level(0)
    spill_up, spill_down = [], []
    for c in range(3):
        for z in range(CZ):
            kc = 3 * z + c
            grid_ref[kc, 0:16, :] += grid_ref[kc, 128:144, :]
            src_ref[z, c] = grid_ref[kc, 0:128, :]

        def b_at(z):
            return src_ref[z, c] if 0 <= z < CZ else 0.0

        for z in range(CZ):
            u_ref[z + 1] = start_of(src_ref[z, c], b_at(z - 1), b_at(z + 1), flat_ring, 0)
        u_ref[0] = (w * w * q) * src_ref[0, c]
        u_ref[CZ + 1] = (w * w * q) * src_ref[CZ - 1, c]

        def left(z):
            if z == -2:
                return q * u_ref[0]
            if z == CZ + 1:
                return q * u_ref[CZ + 1]
            below = u_ref[z] if z > -1 else 0.0
            above = u_ref[z + 2] if z < CZ else 0.0
            return left_of(b_at(z), u_ref[z + 1], below, above, flat_ring, 0)

        rows = []
        for pair in range(-1, 3):
            sum_ref[...] = left(2 * pair) + left(2 * pair + 1)
            rows.append(sum_ref[pl.ds(0, 64, 2), :] + sum_ref[pl.ds(1, 64, 2), :])
        own = dot(rows[1], pool[0]) + dot(rows[2], pool[1])
        up_ref[c] = own
        down_ref[c] = own
        spill_down.append(dot(rows[0], pool[c % 2]))
        spill_up.append(dot(rows[3], pool[c % 2]))
    for ref, far_ref, spill in ((up_ref, up2_ref, spill_up), (down_ref, down2_ref, spill_down)):
        both = spill[0] + spill[1]
        ref[3] = both
        ref[4] = spill[2]
        far_ref[0] = both
        far_ref[1] = spill[2]


def place(meta, payload, fluid):
    return call(
        place_kernel,
        (
            shaped(fluid.shape, F32),
            shaped((5, 64, 128), F32),
            shaped((5, 64, 128), F32),
            shaped((2, 64, 128), F32),
            shaped((2, 64, 128), F32),
            shaped((8, 128), F32),
        ),
        [SMEM, VMEM, VMEM],
        [
            pltpu.VMEM((12, 144, 128), F32),
            pltpu.VMEM((CZ + 2, 128, 128), F32),
            pltpu.VMEM((128, 128), F32),
        ],
    )(meta, near(payload), near(fluid))


def both_layers(tile):
    lane = iota(tile.shape, tile.ndim - 1)
    turned = pltpu.roll(tile, 64, tile.ndim - 1)
    return jnp.where(lane < 64, tile, turned), jnp.where(lane < 64, turned, tile)


def pack_coarse(value):
    last = value[24:32]
    lane = iota((8, 128), 1)
    return [
        jnp.where(lane < 96, value[8 * c : 8 * c + 8], pltpu.roll(last, 96 - 32 * c, 1))
        for c in range(3)
    ]


def unpack_coarse(tile):
    lane = iota((8, 128), 1)
    last = jnp.zeros((8, 128), F32)
    rows = []
    for c in range(3):
        piece = tile[8 * c : 8 * c + 8]
        turned = pltpu.roll(piece, (32 * c - 96) % 128, 1)
        last = jnp.where(lane // 32 == c, turned, last)
        rows.append(jnp.where(lane < 96, piece, 0.0))
    return jnp.concatenate(rows + [last], axis=0)


def spilled(ref, c, first=0):
    return both_layers(ref[first + c // 2])[c % 2]


U_ROW = 9 * 128


def middle_kernel(
    src_ref, up_ref, down_ref, m1_ref, p1_ref, m2_ref, p2_ref,
    pairs_ref, out_ref, rise_ref, sink_ref, sum_ref,
):
    total = None
    for z in range(3):
        for c in range(3):
            rows = slice(128 * (3 * z + c), 128 * (3 * z + c + 1))
            rise_ref[rows, :] = src_ref[z + 1, c]
            sink_ref[rows, :] = src_ref[z, c]
    lane = iota((64, 128), 1)
    for c in range(3):
        m1, own, p1 = both_layers(m1_ref[c]), both_layers(up_ref[c]), both_layers(p1_ref[c])
        b = [
            m1[0] + spilled(m2_ref, c),
            m1[1] + spilled(down_ref, c, 3),
            own[0] + spilled(m1_ref, c, 3),
            own[1] + spilled(p1_ref, c, 3),
            p1[0] + spilled(up_ref, c, 3),
            p1[1] + spilled(p2_ref, c),
        ]
        for j in range(3):
            pairs_ref[j, c] = jnp.where(lane < 64, b[2 * j], b[2 * j + 1])
        u = [start_of(b[i], b[i - 1], b[i + 1], flat_ring, 1) for i in range(1, 5)]
        rows = slice(U_ROW + 64 * c, U_ROW + 64 * c + 64)
        rise_ref[rows, :] = jnp.where(lane < 64, u[0], u[1])
        sink_ref[rows, :] = jnp.where(lane < 64, u[2], u[3])
        left = [left_of(b[i + 1], u[i], u[i - 1], u[i + 1], flat_ring, 1) for i in (1, 2)]
        sum_ref[...] = left[0] + left[1]
        rows = sum_ref[pl.ds(0, 32, 2), :] + sum_ref[pl.ds(1, 32, 2), :]
        pool = jnp.where(
            lanes(lambda r, l: (r // 2 == (l & 31)) & (l // 32 == c) & (r < 64)), 0.125, 0.0
        )
        part = dot(rows, pool)
        total = part if total is None else total + part
    packed = jnp.concatenate(pack_coarse(total), axis=0)
    for d in range(out_ref.shape[0]):
        out_ref[d] = packed


def middle_down(source, up, down, m1, p1, m2, p2):
    return call(
        middle_kernel,
        (
            shaped((3, 3, 64, 128), F32),
            shaped((LOCAL, 24, 128), F32),
            shaped((U_ROW + 192, 128), F32),
            shaped((U_ROW + 192, 128), F32),
        ),
        None,
        [pltpu.VMEM((64, 128), F32)],
    )(*map(near, (source, up, down, m1, p1, m2, p2)))


def inner(x):
    return x[1:-1]


def coarse_part(me, blocks, lift_ref, window_ref, pool_ref, final_ref):
    parity = me % 2
    first = me % LOCAL - parity
    for n, ref in enumerate(blocks):
        window_ref[LOCAL * n : LOCAL * n + LOCAL] = ref[...]
    b2 = jnp.stack([unpack_coarse(window_ref[first + t]) for t in range(34)])
    group = iota((1, 128), 1) // 32
    lift = jnp.zeros((1, 128), F32)
    for c in range(3):
        lift = jnp.where(group == c, lift_ref[c : c + 1, :], lift)
    _, _, w3 = level(3)
    u2 = start_of(inner(b2), b2[:-2], b2[2:], group_ring, 2)
    r2 = left_of(b2[2:-2], inner(u2), u2[:-2], u2[2:], group_ring, 2)
    pairs = r2.reshape(15, 2, 32, 128)
    pool_ref[...] = (pairs[:, 0] + pairs[:, 1]).reshape(480, 128)
    rows = pool_ref[pl.ds(0, 240, 2), :] + pool_ref[pl.ds(1, 240, 2), :]
    pool = jnp.where(
        lanes(lambda r, l: ((r & 31) // 2 == (l & 15)) & (r // 32 == l // 32)), 0.125, 0.0
    )
    b3 = dot(rows, pool).reshape(15, 16, 128)
    u3 = w3 * b3
    for _ in range(5):
        b3 = inner(b3)
        u3 = sweep_of(b3, inner(u3), u3[:-2], u3[2:], group_ring, 3)
    u3 = (u3 + lift[None]).reshape(80, 128)
    spread = jnp.where(
        lanes(lambda r, l: ((l & 31) // 2 == (r & 31)) & (r // 32 == l // 32)), 1.0, 0.0
    )
    wide = dot(u3, spread)
    pool_ref[pl.ds(0, 80, 2), :] = wide
    pool_ref[pl.ds(1, 80, 2), :] = wide
    lifted = pool_ref[0:160, :].reshape(5, 1, 32, 128)
    u = (u2[11:21].reshape(5, 2, 32, 128) + lifted).reshape(10, 32, 128)
    u = sweep_of(b2[13:21], inner(u), u[:-2], u[2:], group_ring, 2)
    u = sweep_of(b2[14:20], inner(u), u[:-2], u[2:], group_ring, 2)
    final_ref[...] = u
    return jnp.concatenate([final_ref[parity + h] for h in range(5)], axis=0)


def up_kernel(
    me_ref, meta_ref, lift_ref, g0_ref, g1_ref, g2_ref, g3_ref, g4_ref,
    pairs_ref, low_ref, own_ref, high_ref, vel_ref, pay_ref,
    window_ref, pool_ref, final_ref, lift1_ref, b1_ref, u1_ref, v1_ref, lift0_ref, u0_ref,
    v0_ref, ext_ref,
):
    blocks = (g0_ref, g1_ref, g2_ref, g3_ref, g4_ref)
    coarse = coarse_part(me_ref[0], blocks, lift_ref, window_ref, pool_ref, final_ref)
    for c in range(3):
        spread = jnp.where(lanes(lambda r, l: r == 32 * c + (l & 63) // 2), 1.0, 0.0)
        wide = dot(coarse, spread)
        lift1_ref[c, pl.ds(0, 160, 2), :] = wide
        lift1_ref[c, pl.ds(1, 160, 2), :] = wide
    spread0 = jnp.where(lanes(lambda r, l: r == l // 2), 1.0, 0.0)

    def b_at(z, c):
        if 0 <= z < CZ:
            return own_ref[z, c]
        ref, first = (low_ref, z + 3) if z < 0 else (high_ref, z - CZ)
        return ref[pl.ds(pl.multiple_of(128 * (3 * first + c), 128), 128), :]

    def component(c, carry):
        for j in range(3):
            b1_ref[2 * j], b1_ref[2 * j + 1] = both_layers(pairs_ref[j, c])
        rows = pl.ds(pl.multiple_of(U_ROW + 64 * c, 64), 64)
        u1 = list(both_layers(low_ref[rows, :]))
        for i in range(1, 5):
            u1.append(start_of(b1_ref[i], b1_ref[i - 1], b1_ref[i + 1], flat_ring, 1))
        u1.extend(both_layers(high_ref[rows, :]))
        for z in range(-3, 5):
            h = z // 2 + 2
            u1_ref[z + 3] = u1[z + 3] + lift1_ref[c, 64 * h : 64 * h + 64, :]
        for z in range(-2, 4):
            i = z + 3
            v1_ref[z + 2] = sweep_of(
                b1_ref[z + 2], u1_ref[i], u1_ref[i - 1], u1_ref[i + 1], flat_ring, 1
            )
        for z in range(-1, 3):
            i = z + 2
            value = sweep_of(
                b1_ref[z + 2], v1_ref[i], v1_ref[i - 1], v1_ref[i + 1], flat_ring, 1
            )
            wide = dot(value, spread0)
            lift0_ref[z + 1, pl.ds(0, 64, 2), :] = wide
            lift0_ref[z + 1, pl.ds(1, 64, 2), :] = wide
        for z in range(-2, 6):
            u0_ref[z + 2] = (
                start_of(b_at(z, c), b_at(z - 1, c), b_at(z + 1, c), flat_ring, 0)
                + lift0_ref[z // 2 + 1]
            )
        for z in range(-1, 5):
            i = z + 2
            v0_ref[z + 1] = sweep_of(
                b_at(z, c), u0_ref[i], u0_ref[i - 1], u0_ref[i + 1], flat_ring, 0
            )
        for z in range(CZ):
            i = z + 1
            value = sweep_of(
                own_ref[z, c], v0_ref[i], v0_ref[i - 1], v0_ref[i + 1], flat_ring, 0
            )
            vel_ref[z, c] = value
            rounded = value.astype(BF16).astype(F32)
            ext_ref[3 * z + c, 0:128, :] = rounded
            ext_ref[3 * z + c, 128:144, :] = rounded[0:16]
        return carry

    lax.fori_loop(0, 3, component, 0)
    lane = iota((8, 128), 1)
    sub = iota((8, 128), 0)

    part = [(lane // BOX) % CZ == k for k in range(CZ)]

    def gather(order, head, base_y):
        base_x = jnp.maximum(head - 1, 0)
        shift = base_x & 7
        row = pl.multiple_of(base_x - shift, 8)
        late = sub >= shift
        values = []
        for k in range(CZ):
            step = (HALF * order + BOX * k - base_y) & 127
            line = []
            for c in range(3):
                tiles = [ext_ref[3 * k + c, pl.ds(row + 8 * n, 8), :] for n in range(3)]
                for n in range(2):
                    value = jnp.where(late, tiles[n], tiles[n + 1])
                    line.append(pltpu.roll(value, step, 1))
            values.append(line)
        return (8 - shift) & 7, values

    group = together(pay_ref.shape[0], 8)

    def several(step, carry):
        found = []
        for n in range(group):
            for order in range(2):
                at = 8 * (step * group + n) + 4 * order
                found.append(gather(order, meta_ref[at], meta_ref[at + 1]))
        for n in range(group):
            pieces = []
            for m in range(6):
                both = []
                for order in range(2):
                    back, values = found[2 * n + order]
                    packed = values[0][m]
                    for k in range(1, CZ):
                        packed = jnp.where(part[k], values[k][m], packed)
                    both.append(pltpu.roll(packed, back, 0))
                pieces.append(jnp.where(lane < HALF, both[0], both[1]))
            pay_ref[step * group + n] = jnp.concatenate(pieces, axis=0).astype(BF16)
        return carry

    lax.fori_loop(0, pay_ref.shape[0] // group, several, 0)


def way_up(me, meta, lift, blocks, pairs, low, own, high, slots):
    return call(
        up_kernel,
        (
            shaped(own.shape, F32, False),
            shaped((slots, ROWS, 128), BF16),
        ),
        [SMEM, SMEM] + [VMEM] * 10,
        [
            pltpu.VMEM((5 * LOCAL, 24, 128), F32),
            pltpu.VMEM((480, 128), F32),
            pltpu.VMEM((6, 32, 128), F32),
            pltpu.VMEM((3, 320, 128), F32),
            pltpu.VMEM((6, 64, 128), F32),
            pltpu.VMEM((8, 64, 128), F32),
            pltpu.VMEM((6, 64, 128), F32),
            pltpu.VMEM((4, 128, 128), F32),
            pltpu.VMEM((8, 128, 128), F32),
            pltpu.VMEM((6, 128, 128), F32),
            pltpu.VMEM((12, 144, 128), F32),
        ],
    )(me, meta, *map(near, (lift, *blocks, pairs, low, own, high)))


def read_kernel(dest_ref, pay_ref, pos_ref, out_ref, stage_ref, count_ref):
    slots = pay_ref.shape[0]

    def widen(t, carry):
        count_ref[t] = 0
        stage_ref[t] = pay_ref[t].astype(F32)
        return carry

    lax.fori_loop(0, slots, widen, 0, unroll=4)
    lane = iota((8, 128), 1)

    group = together(pos_ref.shape[1], 16)

    def one(block, target, order):
        weight_x, weight_y, weight_z = box_weights(pos_ref, block)
        mine = lane // HALF == order
        left = []
        for n in range(6):
            packed = stage_ref[target, 8 * n : 8 * n + 8, :]
            left.append(jnp.where(mine, packed, pltpu.roll(packed, HALF, 1)))
        left = jnp.concatenate(left, axis=0).astype(BF16)
        right = jnp.concatenate(by_levels(weight_y, weight_z), axis=0)
        spread = lax.dot_general(
            left, right, (((1,), (0,)), ((), ())), preferred_element_type=F32
        )
        for c in range(3):
            value = spread[BOX * c : BOX * c + BOX] * weight_x
            out_ref[c, pl.ds(block, 1), :] = jnp.sum(value, axis=0, keepdims=True)

    def several(step, carry):
        places = []
        for n in range(group):
            target = dest_ref[0, step * group + n]
            order = count_ref[target]
            count_ref[target] = order + 1
            places.append((target, order))
        for n in range(group):
            one(step * group + n, *places[n])
        return carry

    lax.fori_loop(0, pos_ref.shape[1] // group, several, 0)


def read(dest, payload, positions):
    slots = payload.shape[0]
    return call(
        read_kernel,
        shaped(positions.shape, F32, False),
        [SMEM, VMEM, VMEM],
        [pltpu.VMEM((slots, ROWS, 128), F32), pltpu.SMEM((slots,), jnp.int32)],
    )(far(dest), near(payload), near(positions))


def moved(value, step):
    size = lax.axis_size(AX)
    return lax.ppermute(value, AX, [(i, (i + step) % size) for i in range(size)])


def exchanged(value, axes=AX):
    return lax.all_to_all(value, axes, split_axis=0, concat_axis=0, tiled=True)


def shards(marker_positions, marker_forces, dest_slab, base_cells, fluid_source):
    slots = lax.axis_size(AX)
    positions = marker_positions.transpose(1, 0, 2)
    forces = marker_forces.transpose(1, 0, 2)
    dest = dest_slab.T
    me = lax.axis_index(AX).astype(jnp.int32).reshape(1)
    payload = exchanged(build(dest, base_cells.T, positions, forces, fluid_source, slots))
    meta = payload[:, 0:1, ::BOX].astype(jnp.int32).reshape(8 * slots)
    source, up, down, up2, down2, lift = place(meta, payload, fluid_source)
    m1, m2 = moved(up, 1), moved(up2, 2)
    p1, p2 = moved(down, -1), moved(down2, -2)
    pairs, share, rise, sink = middle_down(source, up, down, m1, p1, m2, p2)
    middle = exchanged(share, AX[1])
    low, high = moved(rise, 1), moved(sink, -1)
    blocks = [middle if n == 0 else moved(middle, -LOCAL * n) for n in range(-2, 3)]
    velocity, picked = way_up(me, meta, lift, blocks, pairs, low, source, high, slots)
    out = read(dest, exchanged(picked), positions)
    return velocity, out.transpose(1, 0, 2)


def solution(mesh):
    torus = Mesh(mesh.devices.reshape(-1, LOCAL), AX)
    return jax.shard_map(
        shards,
        mesh=torus,
        in_specs=(P(AX), P(AX), P(AX), P(AX), P(AX)),
        out_specs=(P(AX), P(AX)),
        check_vma=False,
    )
```

profile of v0, /device:TPU:1, one launch (start us, length us, event | category | flops | bytes accessed | tf_op | source)
XLA Modules:
  0.0 157.5 jit_solution(1420095127151141481)
XLA Ops:
  0.6 9.8 %shard_map.68 = bf16[128,48,128]{2,1,0:T(8,128)(2,1)S(1)} custom-call(s32[1,128]{1,0:T(1,128)} %bitcast.10, s32[2,128]{1,0:T(2,128)} %bitcast.12, f32[3,128,256]{2,1,0:T(8,128)} %bitcast.6, f32[3,128,256]{2,1,0:T(8,128)} %bitcast.8, f32[4,3,128,128]{3,2,1,0:T(8,128)} %fluid_ref.3), custom_call_target="tpu_custom_call" | custom-call | tf_op jit(solution)/shard_map/pallas_call | solution.py:191
  10.4 0.0 copy-start
  10.4 36.1 %all_to_all.15.pay_ref = bf16[128,48,128]{2,1,0:T(8,128)(2,1)S(1)} all-to-all(bf16[128,48,128]{2,1,0:T(8,128)(2,1)S(1)} %shard_map.68), channel_id=1, replica_groups=mesh['hi'=16,'lo'=8] {'hi','lo'}, dimensions={0} | all-to-all | bytes 3145728 | tf_op jit(solution)/shard_map/all_to_all | solution.py:704
  46.6 1.1 slice.3
  47.7 0.2 convert_reduce_fusion
  47.9 0.1 reshape.16.meta_ref
  48.0 0.0 copy-done
  48.0 7.9 %shard_map.69 = (f32[4,3,128,128]{3,2,1,0:T(8,128)S(1)}, f32[5,64,128]{2,1,0:T(8,128)S(1)}, f32[5,64,128]{2,1,0:T(8,128)S(1)}, f32[2,64,128]{2,1,0:T(8,128)S(1)}...) custom-call(s32[1024]{0:T(1024)S(1)} %reshape.16.meta_ref, bf16[128,48,128]{2,1,0:T(8,128)(2,1)S(1)} %all_to_all.15.pay_ref, ...), custom_call_target="tpu_custom_call" | custom-call | tf_op jit(solution)/shard_map/pallas_call | solution.py:357
  55.9 1.2 collective-permute-start
  57.1 0.0 collective-permute-start.1
  57.1 0.2 collective-permute-start.2
  57.3 6.7 %collective-permute-start.3 = (f32[2,64,128]{2,1,0:T(8,128)S(1)}, f32[2,64,128]{2,1,0:T(8,128)S(1)}, u32[]{:S(2)}, u32[]{:S(2)}) collective-permute-start(f32[2,64,128]{2,1,0:T(8,128)S(1)} %get-tuple-element.19), channel_id=1, source_target_pairs={{0,126},{1,127},{2,0},{3,1},{4,2},{5,3},{6,4},{7,5},{8,6},{9,7},{1... | collective-permute-start | bytes 196616 | tf_op jit(solution)/shard_map/ppermute | solution.py:700
  64.0 3.1 %collective-permute-done.2.m2_ref = f32[2,64,128]{2,1,0:T(8,128)S(1)} collective-permute-done((f32[2,64,128]{2,1,0:T(8,128)S(1)}, f32[2,64,128]{2,1,0:T(8,128)S(1)}, u32[]{:S(2)}, u32[]{:S(2)}) %collective-permute-start.2) | collective-permute-done | bytes 65568 | tf_op jit(solution)/shard_map/ppermute | solution.py:700
  67.1 0.0 collective-permute-done.3.p2_ref
  67.1 0.0 collective-permute-done.m1_ref
  67.1 0.0 collective-permute-done.1.p1_ref
  67.1 2.0 %shard_map.70 = (f32[3,3,64,128]{3,2,1,0:T(8,128)S(1)}, f32[8,24,128]{2,1,0:T(8,128)S(1)}, f32[1344,128]{1,0:T(8,128)}, f32[1344,128]{1,0:T(8,128)}) custom-call(f32[4,3,128,128]{3,2,1,0:T(8,128)S(1)} %get-tuple-element.15.src_ref.own_ref, f32[5,64,128]{2,1,0:T(8,128)S(1)} %get-tuple-element.16.up_ref, f32[5,64,128]{2,1,0:T(8,128)S(1)} %get-tuple-element.17.down_ref, ...), custom_call_target="tpu_custom_call" | custom-call | tf_op jit(solution)/shard_map/pallas_call | solution.py:451
  69.1 0.9 collective-permute-start.8
  70.0 5.8 %collective-permute-start.9 = (f32[1344,128]{1,0:T(8,128)}, f32[1344,128]{1,0:T(8,128)S(1)}, u32[]{:S(2)}, u32[]{:S(2)}) collective-permute-start(f32[1344,128]{1,0:T(8,128)} %get-tuple-element.23), channel_id=1, source_target_pairs={{0,127},{1,0},{2,1},{3,2},{4,3},{5,4},{6,5},{7,6},{8,7},{9,8},{10,... | collective-permute-start | bytes 2064392 | tf_op jit(solution)/shard_map/ppermute | solution.py:700
  75.8 14.8 %all_to_all.16.g2_ref = f32[8,24,128]{2,1,0:T(8,128)S(1)} all-to-all(f32[8,24,128]{2,1,0:T(8,128)S(1)} %get-tuple-element.20), channel_id=1, replica_groups=mesh['hi'=16,'lo'=8] {'lo'}, dimensions={0} | all-to-all | bytes 196608 | tf_op jit(solution)/shard_map/all_to_all | solution.py:704
  90.6 0.0 collective-permute-start.7
  90.6 3.3 %collective-permute-start.6 = (f32[8,24,128]{2,1,0:T(8,128)S(1)}, f32[8,24,128]{2,1,0:T(8,128)S(1)}, u32[]{:S(2)}, u32[]{:S(2)}) collective-permute-start(f32[8,24,128]{2,1,0:T(8,128)S(1)} %all_to_all.16.g2_ref), channel_id=1, source_target_pairs={{0,120},{1,121},{2,122},{3,123},{4,124},{5,125},{6,126},{7,127},{8... | collective-permute-start | bytes 294920 | tf_op jit(solution)/shard_map/ppermute | solution.py:700
  93.9 0.6 collective-permute-start.5
  94.5 1.1 collective-permute-done.7.g4_ref
  95.6 0.7 collective-permute-start.4
  96.3 0.8 collective-permute-done.6.g3_ref
  97.1 3.9 %collective-permute-done.5.g1_ref = f32[8,24,128]{2,1,0:T(8,128)S(1)} collective-permute-done((f32[8,24,128]{2,1,0:T(8,128)S(1)}, f32[8,24,128]{2,1,0:T(8,128)S(1)}, u32[]{:S(2)}, u32[]{:S(2)}) %collective-permute-start.5) | collective-permute-done | bytes 98336 | tf_op jit(solution)/shard_map/ppermute | solution.py:700
  101.0 1.8 %collective-permute-done.4.g0_ref = f32[8,24,128]{2,1,0:T(8,128)S(1)} collective-permute-done((f32[8,24,128]{2,1,0:T(8,128)S(1)}, f32[8,24,128]{2,1,0:T(8,128)S(1)}, u32[]{:S(2)}, u32[]{:S(2)}) %collective-permute-start.4) | collective-permute-done | bytes 98336 | tf_op jit(solution)/shard_map/ppermute | solution.py:700
  102.8 0.0 collective-permute-done.8.low_ref
  102.8 0.0 collective-permute-done.9.high_ref
  102.8 12.5 %shard_map.71 = (f32[4,3,128,128]{3,2,1,0:T(8,128)}, bf16[128,48,128]{2,1,0:T(8,128)(2,1)S(1)}) custom-call(s32[1]{0:T(128)} %bitcast.me_ref, s32[1024]{0:T(1024)S(1)} %reshape.16.meta_ref, f32[8,128]{1,0:T(8,128)S(1)} %get-tuple-element.14.lift_ref, f32[8,24,128]{2,1,0:T(8,128)S(1)} %collective-permute-done.4.g0_ref, ...), custom_call_target="tpu_custom_call" | custom-call | tf_op jit(solution)/shard_map/pallas_call | solution.py:622
  115.3 0.0 copy-start.1
  115.3 35.0 %all_to_all.17.pay_ref = bf16[128,48,128]{2,1,0:T(8,128)(2,1)S(1)} all-to-all(bf16[128,48,128]{2,1,0:T(8,128)(2,1)S(1)} %get-tuple-element.25), channel_id=1, replica_groups=mesh['hi'=16,'lo'=8] {'hi','lo'}, dimensions={0} | all-to-all | bytes 3145728 | tf_op jit(solution)/shard_map/all_to_all | solution.py:704
  150.3 0.0 copy-done.1
  150.3 7.2 %shard_map.72 = f32[3,128,256]{2,1,0:T(8,128)} custom-call(s32[1,128]{1,0:T(1,128)} %bitcast.11, bf16[128,48,128]{2,1,0:T(8,128)(2,1)S(1)} %all_to_all.17.pay_ref, f32[3,128,256]{2,1,0:T(8,128)S(1)} %bitcast.7), custom_call_target="tpu_custom_call" | custom-call | tf_op jit(solution)/shard_map/pallas_call | solution.py:690
Async XLA Ops:
  10.4 37.6 %copy-start = (f32[4,3,128,128]{3,2,1,0:T(8,128)S(1)}, f32[4,3,128,128]{3,2,1,0:T(8,128)}, u32[]{:S(2)}) copy-start(f32[4,3,128,128]{3,2,1,0:T(8,128)} %fluid_ref.3) | copy-start | bytes 2359300
  55.9 11.2 %collective-permute-start = (f32[5,64,128]{2,1,0:T(8,128)S(1)}, f32[5,64,128]{2,1,0:T(8,128)S(1)}, u32[]{:S(2)}, u32[]{:S(2)}) collective-permute-start(f32[5,64,128]{2,1,0:T(8,128)S(1)} %get-tuple-element.16.up_ref), channel_id=1, source_target_pairs={{0,1},{1,2},{2,3},{3,4},{4,5},{5,6},{6,7},{7,8},{8,9},{9,10},{10,1... | collective-permute-start | bytes 491528 | tf_op jit(solution)/shard_map/ppermute | solution.py:700
  57.1 10.0 %collective-permute-start.1 = (f32[5,64,128]{2,1,0:T(8,128)S(1)}, f32[5,64,128]{2,1,0:T(8,128)S(1)}, u32[]{:S(2)}, u32[]{:S(2)}) collective-permute-start(f32[5,64,128]{2,1,0:T(8,128)S(1)} %get-tuple-element.17.down_ref), channel_id=1, source_target_pairs={{0,127},{1,0},{2,1},{3,2},{4,3},{5,4},{6,5},{7,6},{8,7},{9,8},{10,... | collective-permute-start | bytes 491528 | tf_op jit(solution)/shard_map/ppermute | solution.py:700
  57.1 10.0 %collective-permute-start.2 = (f32[2,64,128]{2,1,0:T(8,128)S(1)}, f32[2,64,128]{2,1,0:T(8,128)S(1)}, u32[]{:S(2)}, u32[]{:S(2)}) collective-permute-start(f32[2,64,128]{2,1,0:T(8,128)S(1)} %get-tuple-element.18), channel_id=1, source_target_pairs={{0,2},{1,3},{2,4},{3,5},{4,6},{5,7},{6,8},{7,9},{8,10},{9,11},{10,... | collective-permute-start | bytes 196616 | tf_op jit(solution)/shard_map/ppermute | solution.py:700
  57.3 9.8 %collective-permute-start.3 = (f32[2,64,128]{2,1,0:T(8,128)S(1)}, f32[2,64,128]{2,1,0:T(8,128)S(1)}, u32[]{:S(2)}, u32[]{:S(2)}) collective-permute-start(f32[2,64,128]{2,1,0:T(8,128)S(1)} %get-tuple-element.19), channel_id=1, source_target_pairs={{0,126},{1,127},{2,0},{3,1},{4,2},{5,3},{6,4},{7,5},{8,6},{9,7},{1... | collective-permute-start | bytes 196616 | tf_op jit(solution)/shard_map/ppermute | solution.py:700
  69.1 33.7 %collective-permute-start.8 = (f32[1344,128]{1,0:T(8,128)}, f32[1344,128]{1,0:T(8,128)S(1)}, u32[]{:S(2)}, u32[]{:S(2)}) collective-permute-start(f32[1344,128]{1,0:T(8,128)} %get-tuple-element.22), channel_id=1, source_target_pairs={{0,1},{1,2},{2,3},{3,4},{4,5},{5,6},{6,7},{7,8},{8,9},{9,10},{10,1... | collective-permute-start | bytes 2064392 | tf_op jit(solution)/shard_map/ppermute | solution.py:700
  70.0 32.8 %collective-permute-start.9 = (f32[1344,128]{1,0:T(8,128)}, f32[1344,128]{1,0:T(8,128)S(1)}, u32[]{:S(2)}, u32[]{:S(2)}) collective-permute-start(f32[1344,128]{1,0:T(8,128)} %get-tuple-element.23), channel_id=1, source_target_pairs={{0,127},{1,0},{2,1},{3,2},{4,3},{5,4},{6,5},{7,6},{8,7},{9,8},{10,... | collective-permute-start | bytes 2064392 | tf_op jit(solution)/shard_map/ppermute | solution.py:700
  90.6 5.0 %collective-permute-start.7 = (f32[8,24,128]{2,1,0:T(8,128)S(1)}, f32[8,24,128]{2,1,0:T(8,128)S(1)}, u32[]{:S(2)}, u32[]{:S(2)}) collective-permute-start(f32[8,24,128]{2,1,0:T(8,128)S(1)} %all_to_all.16.g2_ref), channel_id=1, source_target_pairs={{0,112},{1,113},{2,114},{3,115},{4,116},{5,117},{6,118},{7,119},{8... | collective-permute-start | bytes 294920 | tf_op jit(solution)/shard_map/ppermute | solution.py:700
  90.6 6.5 %collective-permute-start.6 = (f32[8,24,128]{2,1,0:T(8,128)S(1)}, f32[8,24,128]{2,1,0:T(8,128)S(1)}, u32[]{:S(2)}, u32[]{:S(2)}) collective-permute-start(f32[8,24,128]{2,1,0:T(8,128)S(1)} %all_to_all.16.g2_ref), channel_id=1, source_target_pairs={{0,120},{1,121},{2,122},{3,123},{4,124},{5,125},{6,126},{7,127},{8... | collective-permute-start | bytes 294920 | tf_op jit(solution)/shard_map/ppermute | solution.py:700
  93.9 7.1 %collective-permute-start.5 = (f32[8,24,128]{2,1,0:T(8,128)S(1)}, f32[8,24,128]{2,1,0:T(8,128)S(1)}, u32[]{:S(2)}, u32[]{:S(2)}) collective-permute-start(f32[8,24,128]{2,1,0:T(8,128)S(1)} %all_to_all.16.g2_ref), channel_id=1, source_target_pairs={{0,8},{1,9},{2,10},{3,11},{4,12},{5,13},{6,14},{7,15},{8,16},{9,17... | collective-permute-start | bytes 294920 | tf_op jit(solution)/shard_map/ppermute | solution.py:700
  95.6 7.2 %collective-permute-start.4 = (f32[8,24,128]{2,1,0:T(8,128)S(1)}, f32[8,24,128]{2,1,0:T(8,128)S(1)}, u32[]{:S(2)}, u32[]{:S(2)}) collective-permute-start(f32[8,24,128]{2,1,0:T(8,128)S(1)} %all_to_all.16.g2_ref), channel_id=1, source_target_pairs={{0,16},{1,17},{2,18},{3,19},{4,20},{5,21},{6,22},{7,23},{8,24},{9,... | collective-permute-start | bytes 294920 | tf_op jit(solution)/shard_map/ppermute | solution.py:700
  115.3 35.0 %copy-start.1 = (f32[128,3,256]{2,0,1:T(8,128)S(1)}, f32[128,3,256]{2,0,1:T(8,128)}, u32[]{:S(2)}) copy-start(f32[128,3,256]{2,0,1:T(8,128)} %param.5) | copy-start | bytes 1179652
where the time goes:
time: 158 us
  blocking collectives  86 us (54%)
  Pallas kernels  39.4 us (25%)
  starting transfers between devices  19.4 us (12%)
  waiting for transfers between devices  10.7 us (7%)
    all_to_all x3, blocking collectives, exchanged(): return lax.all_to_all(value, axes, split_axis=0, concat_axis=0, tiled=True)  86 us
    ppermute x10, starting transfers between devices, moved(): lax.ppermute(value, AX, [(i, (i + step) % size) for i in range(size)])  19.4 us
    pallas_call x1, Pallas kernels, way_up(): call(up_kernel, (shaped(own.shape, F32, False), shaped((slots, ROWS, 128)...  12.5 us
    ppermute x10, waiting for transfers between devices, moved(): lax.ppermute(value, AX, [(i, (i + step) % size) for i in range(size)])  10.7 us
    pallas_call x1, Pallas kernels, build(): call(build_kernel, shaped((slots, ROWS, 128), BF16), [SMEM, SMEM, VMEM, V...  9.78 us
    pallas_call x1, Pallas kernels, place(): call(place_kernel, (shaped(fluid.shape, F32), shaped((5, 64, 128), F32),...  7.91 us
    pallas_call x1, Pallas kernels, read(): call(read_kernel, shaped(positions.shape, F32, False), [SMEM, VMEM, VMEM]...  7.21 us
  transfers between devices with their start and end apart: 10, of which 5 were waited for; matrix products, arithmetic and copies ran while one was open for 0% of the time, Pallas kernels for 0%

commit v1 on v0

--- a/solution.py
+++ b/solution.py
@@ -62,21 +62,26 @@
 
 
 COS = (
-    0.13884009367929634,
-    0.008677498753340366,
-    0.0001925760632832398,
-    2.2059131886721028e-06,
-    1.644977822379996e-08,
+    0.9999999999524891,
+    -1.2337005406331254,
+    0.2536692036544627,
+    -0.02086006949632079,
+    0.0009036280586426939,
 )
-
-
-def phi(offset):
-    inside = jnp.maximum(4.0 - offset * offset, 0.0)
-    value = inside * COS[-1] + COS[-2]
-    for coefficient in COS[-3::-1]:
-        value = value * inside + coefficient
-    value = value * inside
-    return value * value
+SIN = (
+    1.5707963267880989,
+    -0.6459640961467292,
+    0.07969258272440714,
+    -0.004681266248964948,
+    0.00015820628792786513,
+)
+
+
+def polynomial(coefficients, x):
+    value = x * coefficients[-1] + coefficients[-2]
+    for coefficient in coefficients[-3::-1]:
+        value = value * x + coefficient
+    return value
 
 
 def split(value):
@@ -84,14 +89,39 @@
     return high, (value - high.astype(F32)).astype(BF16)
 
 
-def box_weights(pos_ref, block):
-    cells = iota((BOX, 256), 0).astype(F32)
-    levels = iota((8, 256), 0).astype(F32)
-    row = pl.ds(block, 1)
-    along_x = 2.0 + (BOX - 5) * pos_ref[0, row, :]
-    along_y = 2.0 + (BOX - 5) * pos_ref[1, row, :]
-    height = (CZ - 1) * pos_ref[2, row, :]
-    return phi(along_x - cells), phi(along_y - cells), phi(height - levels)
+def waves(pos_ref, first, group, wave_ref):
+    rows = pl.ds(pl.multiple_of(first, group), group)
+    for axis in range(3):
+        point = pos_ref[axis, rows, :]
+        point = 2.0 + (BOX - 5) * point if axis < 2 else (CZ - 1) * point
+        nearest = jnp.floor(point + 0.5)
+        rest = point - nearest
+        square = rest * rest
+        even = polynomial(COS, square)
+        odd = polynomial(SIN, square) * rest
+        quarter = nearest.astype(jnp.int32) & 3
+        swap = (quarter & 1) == 1
+        cosine = jnp.where(swap, odd, even)
+        sine = jnp.where(swap, even, odd)
+        wave_ref[3 * axis] = point
+        wave_ref[3 * axis + 1] = jnp.where((quarter == 1) | (quarter == 2), -cosine, cosine)
+        wave_ref[3 * axis + 2] = jnp.where(quarter >= 2, -sine, sine)
+
+
+def box_weights(wave_ref, block):
+    row = slice(block, block + 1)
+    cell = iota((8, 256), 0)
+    sign = jnp.where(cell % 4 < 2, 0.25, -0.25)
+    weights = []
+    for axis in range(3):
+        point, cosine, sine = (wave_ref[3 * axis + n, row, :] for n in range(3))
+        pattern = jnp.where(cell % 2 == 0, cosine, sine) * sign + 0.25
+        parts = []
+        for first in range(0, BOX if axis < 2 else 8, 8):
+            offset = point - (cell + first).astype(F32)
+            parts.append(jnp.where(jnp.abs(offset) < 2.0, pattern, 0.0))
+        weights.append(jnp.concatenate(parts, axis=0) if axis < 2 else parts[0])
+    return weights
 
 
 def by_levels(weight_y, weight_z):
@@ -106,7 +136,7 @@
 
 
 def build_kernel(
-    dest_ref, base_ref, pos_ref, frc_ref, fluid_ref, out_ref, stage_ref, count_ref
+    dest_ref, base_ref, pos_ref, frc_ref, fluid_ref, out_ref, stage_ref, count_ref, wave_ref
 ):
     slots = out_ref.shape[0]
     blocks = pos_ref.shape[1]
@@ -121,8 +151,9 @@
     lane = iota((8, 128), 1)
     top = iota((8, 128), 0) == 0
 
-    def one(block):
-        weight_x, weight_y, weight_z = box_weights(pos_ref, block)
+    def one(first, n):
+        block = first + n
+        weight_x, weight_y, weight_z = box_weights(wave_ref, n)
         loaded = [frc_ref[c, pl.ds(block, 1), :] * weight_x for c in range(3)]
         high, low = split(jnp.concatenate(loaded, axis=0))
         right = jnp.concatenate(by_levels(weight_y, weight_z), axis=0)
@@ -141,8 +172,9 @@
 
     def several(step, carry):
         results = []
+        waves(pos_ref, step * group, group, wave_ref)
         for n in range(group):
-            tiles, sums = one(step * group + n)
+            tiles, sums = one(step * group, n)
             results.append(tiles)
             carry = tuple(a + b for a, b in zip(carry, sums))
         for n in range(group):
@@ -192,7 +224,11 @@
         build_kernel,
         shaped((slots, ROWS, 128), BF16),
         [SMEM, SMEM, VMEM, VMEM, VMEM],
-        [pltpu.VMEM((slots, ROWS, 128), F32), pltpu.SMEM((slots,), jnp.int32)],
+        [
+            pltpu.VMEM((slots, ROWS, 128), F32),
+            pltpu.SMEM((slots,), jnp.int32),
+            pltpu.VMEM((9, together(positions.shape[1], 16), 256), F32),
+        ],
     )(*map(far, (dest, base, positions, forces, fluid)))
 
 
@@ -404,7 +440,7 @@
     return both_layers(ref[first + c // 2])[c % 2]
 
 
-U_ROW = 9 * 128
+U_ROW = 12 * 128
 
 
 def middle_kernel(
@@ -412,11 +448,12 @@
     pairs_ref, out_ref, rise_ref, sink_ref, sum_ref,
 ):
     total = None
-    for z in range(3):
+    for ref, order in ((rise_ref, (3, 2, 1)), (sink_ref, (0, 1, 2))):
         for c in range(3):
-            rows = slice(128 * (3 * z + c), 128 * (3 * z + c + 1))
-            rise_ref[rows, :] = src_ref[z + 1, c]
-            sink_ref[rows, :] = src_ref[z, c]
+            parts = split(src_ref[order[0], c])
+            parts += tuple(src_ref[z, c].astype(BF16) for z in order[1:])
+            for n in range(4):
+                ref[128 * (3 * n + c) : 128 * (3 * n + c + 1), :] = parts[n]
     lane = iota((64, 128), 1)
     for c in range(3):
         m1, own, p1 = both_layers(m1_ref[c]), both_layers(up_ref[c]), both_layers(p1_ref[c])
@@ -432,8 +469,8 @@
             pairs_ref[j, c] = jnp.where(lane < 64, b[2 * j], b[2 * j + 1])
         u = [start_of(b[i], b[i - 1], b[i + 1], flat_ring, 1) for i in range(1, 5)]
         rows = slice(U_ROW + 64 * c, U_ROW + 64 * c + 64)
-        rise_ref[rows, :] = jnp.where(lane < 64, u[0], u[1])
-        sink_ref[rows, :] = jnp.where(lane < 64, u[2], u[3])
+        rise_ref[rows, :] = jnp.where(lane < 64, u[0], u[1]).astype(BF16)
+        sink_ref[rows, :] = jnp.where(lane < 64, u[2], u[3]).astype(BF16)
         left = [left_of(b[i + 1], u[i], u[i - 1], u[i + 1], flat_ring, 1) for i in (1, 2)]
         sum_ref[...] = left[0] + left[1]
         rows = sum_ref[pl.ds(0, 32, 2), :] + sum_ref[pl.ds(1, 32, 2), :]
@@ -453,8 +490,8 @@
         (
             shaped((3, 3, 64, 128), F32),
             shaped((LOCAL, 24, 128), F32),
-            shaped((U_ROW + 192, 128), F32),
-            shaped((U_ROW + 192, 128), F32),
+            shaped((U_ROW + 192, 128), BF16),
+            shaped((U_ROW + 192, 128), BF16),
         ),
         None,
         [pltpu.VMEM((64, 128), F32)],
@@ -508,7 +545,7 @@
     me_ref, meta_ref, lift_ref, g0_ref, g1_ref, g2_ref, g3_ref, g4_ref,
     pairs_ref, low_ref, own_ref, high_ref, vel_ref, pay_ref,
     window_ref, pool_ref, final_ref, lift1_ref, b1_ref, u1_ref, v1_ref, lift0_ref, u0_ref,
-    v0_ref, ext_ref,
+    v0_ref, ext_ref, halo_ref,
 ):
     blocks = (g0_ref, g1_ref, g2_ref, g3_ref, g4_ref)
     coarse = coarse_part(me_ref[0], blocks, lift_ref, window_ref, pool_ref, final_ref)
@@ -522,17 +559,24 @@
     def b_at(z, c):
         if 0 <= z < CZ:
             return own_ref[z, c]
-        ref, first = (low_ref, z + 3) if z < 0 else (high_ref, z - CZ)
-        return ref[pl.ds(pl.multiple_of(128 * (3 * first + c), 128), 128), :]
+        return halo_ref[z + 3 if z < 0 else z - 1]
 
     def component(c, carry):
+        for ref, order in ((low_ref, (2, 1, 0)), (high_ref, (3, 4, 5))):
+            planes = [
+                ref[pl.ds(pl.multiple_of(128 * (3 * n + c), 128), 128), :].astype(F32)
+                for n in range(4)
+            ]
+            halo_ref[order[0]] = planes[0] + planes[1]
+            halo_ref[order[1]] = planes[2]
+            halo_ref[order[2]] = planes[3]
         for j in range(3):
             b1_ref[2 * j], b1_ref[2 * j + 1] = both_layers(pairs_ref[j, c])
         rows = pl.ds(pl.multiple_of(U_ROW + 64 * c, 64), 64)
-        u1 = list(both_layers(low_ref[rows, :]))
+        u1 = list(both_layers(low_ref[rows, :].astype(F32)))
         for i in range(1, 5):
             u1.append(start_of(b1_ref[i], b1_ref[i - 1], b1_ref[i + 1], flat_ring, 1))
-        u1.extend(both_layers(high_ref[rows, :]))
+        u1.extend(both_layers(high_ref[rows, :].astype(F32)))
         for z in range(-3, 5):
             h = z // 2 + 2
             u1_ref[z + 3] = u1[z + 3] + lift1_ref[c, 64 * h : 64 * h + 64, :]
@@ -638,11 +682,12 @@
             pltpu.VMEM((8, 128, 128), F32),
             pltpu.VMEM((6, 128, 128), F32),
             pltpu.VMEM((12, 144, 128), F32),
+            pltpu.VMEM((6, 128, 128), F32),
         ],
     )(me, meta, *map(near, (lift, *blocks, pairs, low, own, high)))
 
 
-def read_kernel(dest_ref, pay_ref, pos_ref, out_ref, stage_ref, count_ref):
+def read_kernel(dest_ref, pay_ref, pos_ref, out_ref, stage_ref, count_ref, wave_ref):
     slots = pay_ref.shape[0]
 
     def widen(t, carry):
@@ -655,12 +700,13 @@
 
     group = together(pos_ref.shape[1], 16)
 
-    def one(block, target, order):
-        weight_x, weight_y, weight_z = box_weights(pos_ref, block)
+    def one(first, n, target, order):
+        block = first + n
+        weight_x, weight_y, weight_z = box_weights(wave_ref, n)
         mine = lane // HALF == order
         left = []
-        for n in range(6):
-            packed = stage_ref[target, 8 * n : 8 * n + 8, :]
+        for m in range(6):
+            packed = stage_ref[target, 8 * m : 8 * m + 8, :]
             left.append(jnp.where(mine, packed, pltpu.roll(packed, HALF, 1)))
         left = jnp.concatenate(left, axis=0).astype(BF16)
         right = jnp.concatenate(by_levels(weight_y, weight_z), axis=0)
@@ -678,8 +724,9 @@
             order = count_ref[target]
             count_ref[target] = order + 1
             places.append((target, order))
+        waves(pos_ref, step * group, group, wave_ref)
         for n in range(group):
-            one(step * group + n, *places[n])
+            one(step * group, n, *places[n])
         return carry
 
     lax.fori_loop(0, pos_ref.shape[1] // group, several, 0)
@@ -691,7 +738,11 @@
         read_kernel,
         shaped(positions.shape, F32, False),
         [SMEM, VMEM, VMEM],
-        [pltpu.VMEM((slots, ROWS, 128), F32), pltpu.SMEM((slots,), jnp.int32)],
+        [
+            pltpu.VMEM((slots, ROWS, 128), F32),
+            pltpu.SMEM((slots,), jnp.int32),
+            pltpu.VMEM((9, together(positions.shape[1], 16), 256), F32),
+        ],
     )(far(dest), near(payload), near(positions))
 
 

time: 158 us -> 154 us (0.975)
  starting transfers between devices: 19.4 us -> 16.4 us
  waiting for transfers between devices: 10.7 us -> 13.6 us
  blocking collectives: 86 us -> 83.4 us
    ppermute x10, starting transfers between devices: 19.4 us -> 16.4 us  [moved(): lax.ppermute(value, AX, [(i, (i + step) % size) for i in range(size)])]
    ppermute x10, waiting for transfers between devices: 10.7 us -> 13.6 us  [moved(): lax.ppermute(value, AX, [(i, (i + step) % size) for i in range(size)])]
    all_to_all x3, blocking collectives: 86 us -> 83.4 us  [exchanged(): return lax.all_to_all(value, axes, split_axis=0, concat_axis=0, tiled=True)]
  transfers between devices with their start and end apart: 10 -> 10, of which waited for: 5 -> 4; matrix products, arithmetic and copies ran while one was open for 0% -> 0% of each run, Pallas kernels for 0% -> 0%
where the time goes in v1:
time: 154 us
  blocking collectives  83.4 us (54%)
  Pallas kernels  38.3 us (25%)
  starting transfers between devices  16.4 us (11%)
  waiting for transfers between devices  13.6 us (9%)
    all_to_all x3, blocking collectives, exchanged(): return lax.all_to_all(value, axes, split_axis=0, concat_axis=0, tiled=True)  83.4 us
    ppermute x10, starting transfers between devices, moved(): lax.ppermute(value, AX, [(i, (i + step) % size) for i in range(size)])  16.4 us
    ppermute x10, waiting for transfers between devices, moved(): lax.ppermute(value, AX, [(i, (i + step) % size) for i in range(size)])  13.6 us
    pallas_call x1, Pallas kernels, way_up(): call(up_kernel, (shaped(own.shape, F32, False), shaped((slots, ROWS, 128)...  12.5 us
    pallas_call x1, Pallas kernels, build(): call(build_kernel, shaped((slots, ROWS, 128), BF16), [SMEM, SMEM, VMEM, V...  9.87 us
    pallas_call x1, Pallas kernels, place(): call(place_kernel, (shaped(fluid.shape, F32), shaped((5, 64, 128), F32),...  7.91 us
    pallas_call x1, Pallas kernels, read(): call(read_kernel, shaped(positions.shape, F32, False), [SMEM, VMEM, VMEM]...  6.29 us
  transfers between devices with their start and end apart: 10, of which 4 were waited for; matrix products, arithmetic and copies ran while one was open for 0% of the time, Pallas kernels for 0%

profile of v1, /device:TPU:1, one launch (start us, length us, event | category | flops | bytes accessed | tf_op | source)
XLA Modules:
  0.0 153.8 jit_solution(15448708707730026850)
XLA Ops:
  0.6 9.9 %shard_map.68 = bf16[128,48,128]{2,1,0:T(8,128)(2,1)S(1)} custom-call(s32[1,128]{1,0:T(1,128)} %bitcast.10, s32[2,128]{1,0:T(2,128)} %bitcast.12, f32[3,128,256]{2,1,0:T(8,128)} %bitcast.6, f32[3,128,256]{2,1,0:T(8,128)} %bitcast.8, f32[4,3,128,128]{3,2,1,0:T(8,128)} %fluid_ref.3), custom_call_target="tpu_custom_call" | custom-call | tf_op jit(solution)/shard_map/pallas_call | solution.py:223
  10.5 0.0 copy-start
  10.5 36.1 %all_to_all.15.pay_ref = bf16[128,48,128]{2,1,0:T(8,128)(2,1)S(1)} all-to-all(bf16[128,48,128]{2,1,0:T(8,128)(2,1)S(1)} %shard_map.68), channel_id=1, replica_groups=mesh['hi'=16,'lo'=8] {'hi','lo'}, dimensions={0} | all-to-all | bytes 3145728 | tf_op jit(solution)/shard_map/all_to_all | solution.py:755
  46.7 1.1 slice.3
  47.8 0.2 convert_reduce_fusion
  48.0 0.1 reshape.16.meta_ref
  48.1 0.0 copy-done
  48.1 7.9 %shard_map.69 = (f32[4,3,128,128]{3,2,1,0:T(8,128)S(1)}, f32[5,64,128]{2,1,0:T(8,128)S(1)}, f32[5,64,128]{2,1,0:T(8,128)S(1)}, f32[2,64,128]{2,1,0:T(8,128)S(1)}...) custom-call(s32[1024]{0:T(1024)S(1)} %reshape.16.meta_ref, bf16[128,48,128]{2,1,0:T(8,128)(2,1)S(1)} %all_to_all.15.pay_ref, ...), custom_call_target="tpu_custom_call" | custom-call | tf_op jit(solution)/shard_map/pallas_call | solution.py:393
  56.0 1.2 collective-permute-start
  57.2 0.0 collective-permute-start.1
  57.2 0.2 collective-permute-start.2
  57.4 6.7 %collective-permute-start.3 = (f32[2,64,128]{2,1,0:T(8,128)S(1)}, f32[2,64,128]{2,1,0:T(8,128)S(1)}, u32[]{:S(2)}, u32[]{:S(2)}) collective-permute-start(f32[2,64,128]{2,1,0:T(8,128)S(1)} %get-tuple-element.19), channel_id=1, source_target_pairs={{0,126},{1,127},{2,0},{3,1},{4,2},{5,3},{6,4},{7,5},{8,6},{9,7},{1... | collective-permute-start | bytes 196616 | tf_op jit(solution)/shard_map/ppermute | solution.py:751
  64.1 3.1 %collective-permute-done.2.m2_ref = f32[2,64,128]{2,1,0:T(8,128)S(1)} collective-permute-done((f32[2,64,128]{2,1,0:T(8,128)S(1)}, f32[2,64,128]{2,1,0:T(8,128)S(1)}, u32[]{:S(2)}, u32[]{:S(2)}) %collective-permute-start.2) | collective-permute-done | bytes 65568 | tf_op jit(solution)/shard_map/ppermute | solution.py:751
  67.2 0.0 collective-permute-done.3.p2_ref
  67.2 0.0 collective-permute-done.m1_ref
  67.2 0.0 collective-permute-done.1.p1_ref
  67.2 1.7 %shard_map.70 = (f32[3,3,64,128]{3,2,1,0:T(8,128)S(1)}, f32[8,24,128]{2,1,0:T(8,128)S(1)}, bf16[1728,128]{1,0:T(8,128)(2,1)}, bf16[1728,128]{1,0:T(8,128)(2,1)S(1)}) custom-call(f32[4,3,128,128]{3,2,1,0:T(8,128)S(1)} %get-tuple-element.15.src_ref.own_ref, f32[5,64,128]{2,1,0:T(8,128)S(1)} %get-tuple-element.16.up_ref, ...), custom_call_target="tpu_custom_call" | custom-call | tf_op jit(solution)/shard_map/pallas_call | solution.py:488
  68.9 0.9 collective-permute-start.8
  69.8 5.8 %collective-permute-start.9 = (bf16[1728,128]{1,0:T(8,128)(2,1)S(1)}, bf16[1728,128]{1,0:T(8,128)(2,1)S(1)}, u32[]{:S(2)}, u32[]{:S(2)}) collective-permute-start(bf16[1728,128]{1,0:T(8,128)(2,1)S(1)} %get-tuple-element.23), channel_id=1, source_target_pairs={{0,127},{1,0},{2,1},{3,2},{4,3},{5,4},{6,5},{7,6},{8,7},{9,8},{10,... | collective-permute-start | bytes 1327112 | tf_op jit(solution)/shard_map/ppermute | solution.py:751
  75.6 14.5 %all_to_all.16.g2_ref = f32[8,24,128]{2,1,0:T(8,128)S(1)} all-to-all(f32[8,24,128]{2,1,0:T(8,128)S(1)} %get-tuple-element.20), channel_id=1, replica_groups=mesh['hi'=16,'lo'=8] {'lo'}, dimensions={0} | all-to-all | bytes 196608 | tf_op jit(solution)/shard_map/all_to_all | solution.py:755
  90.1 0.0 collective-permute-start.7
  90.1 1.0 collective-permute-start.6
  91.1 0.6 collective-permute-start.5
  91.7 3.4 %collective-permute-done.7.g4_ref = f32[8,24,128]{2,1,0:T(8,128)S(1)} collective-permute-done((f32[8,24,128]{2,1,0:T(8,128)S(1)}, f32[8,24,128]{2,1,0:T(8,128)S(1)}, u32[]{:S(2)}, u32[]{:S(2)}) %collective-permute-start.7) | collective-permute-done | bytes 98336 | tf_op jit(solution)/shard_map/ppermute | solution.py:751
  95.1 0.0 collective-permute-start.4
  95.1 0.0 collective-permute-done.6.g3_ref
  95.1 3.0 %collective-permute-done.5.g1_ref = f32[8,24,128]{2,1,0:T(8,128)S(1)} collective-permute-done((f32[8,24,128]{2,1,0:T(8,128)S(1)}, f32[8,24,128]{2,1,0:T(8,128)S(1)}, u32[]{:S(2)}, u32[]{:S(2)}) %collective-permute-start.5) | collective-permute-done | bytes 98336 | tf_op jit(solution)/shard_map/ppermute | solution.py:751
  98.1 4.1 %collective-permute-done.4.g0_ref = f32[8,24,128]{2,1,0:T(8,128)S(1)} collective-permute-done((f32[8,24,128]{2,1,0:T(8,128)S(1)}, f32[8,24,128]{2,1,0:T(8,128)S(1)}, u32[]{:S(2)}, u32[]{:S(2)}) %collective-permute-start.4) | collective-permute-done | bytes 98336 | tf_op jit(solution)/shard_map/ppermute | solution.py:751
  102.2 0.0 collective-permute-done.8.low_ref
  102.2 0.0 collective-permute-done.9.high_ref
  102.2 12.5 %shard_map.71 = (f32[4,3,128,128]{3,2,1,0:T(8,128)}, bf16[128,48,128]{2,1,0:T(8,128)(2,1)S(1)}) custom-call(s32[1]{0:T(128)} %bitcast.me_ref, s32[1024]{0:T(1024)S(1)} %reshape.16.meta_ref, f32[8,128]{1,0:T(8,128)S(1)} %get-tuple-element.14.lift_ref, f32[8,24,128]{2,1,0:T(8,128)S(1)} %collective-permute-done.4.g0_ref, ...), custom_call_target="tpu_custom_call" | custom-call | tf_op jit(solution)/shard_map/pallas_call | solution.py:666
  114.7 0.0 copy-start.1
  114.7 32.7 %all_to_all.17.pay_ref = bf16[128,48,128]{2,1,0:T(8,128)(2,1)S(1)} all-to-all(bf16[128,48,128]{2,1,0:T(8,128)(2,1)S(1)} %get-tuple-element.25), channel_id=1, replica_groups=mesh['hi'=16,'lo'=8] {'hi','lo'}, dimensions={0} | all-to-all | bytes 3145728 | tf_op jit(solution)/shard_map/all_to_all | solution.py:755
  147.5 0.0 copy-done.1
  147.5 6.3 %shard_map.72 = f32[3,128,256]{2,1,0:T(8,128)} custom-call(s32[1,128]{1,0:T(1,128)} %bitcast.11, bf16[128,48,128]{2,1,0:T(8,128)(2,1)S(1)} %all_to_all.17.pay_ref, f32[3,128,256]{2,1,0:T(8,128)S(1)} %bitcast.7), custom_call_target="tpu_custom_call" | custom-call | tf_op jit(solution)/shard_map/pallas_call | solution.py:737
Async XLA Ops:
  10.5 37.6 %copy-start = (f32[4,3,128,128]{3,2,1,0:T(8,128)S(1)}, f32[4,3,128,128]{3,2,1,0:T(8,128)}, u32[]{:S(2)}) copy-start(f32[4,3,128,128]{3,2,1,0:T(8,128)} %fluid_ref.3) | copy-start | bytes 2359300
  56.0 11.2 %collective-permute-start = (f32[5,64,128]{2,1,0:T(8,128)S(1)}, f32[5,64,128]{2,1,0:T(8,128)S(1)}, u32[]{:S(2)}, u32[]{:S(2)}) collective-permute-start(f32[5,64,128]{2,1,0:T(8,128)S(1)} %get-tuple-element.16.up_ref), channel_id=1, source_target_pairs={{0,1},{1,2},{2,3},{3,4},{4,5},{5,6},{6,7},{7,8},{8,9},{9,10},{10,1... | collective-permute-start | bytes 491528 | tf_op jit(solution)/shard_map/ppermute | solution.py:751
  57.2 10.0 %collective-permute-start.1 = (f32[5,64,128]{2,1,0:T(8,128)S(1)}, f32[5,64,128]{2,1,0:T(8,128)S(1)}, u32[]{:S(2)}, u32[]{:S(2)}) collective-permute-start(f32[5,64,128]{2,1,0:T(8,128)S(1)} %get-tuple-element.17.down_ref), channel_id=1, source_target_pairs={{0,127},{1,0},{2,1},{3,2},{4,3},{5,4},{6,5},{7,6},{8,7},{9,8},{10,... | collective-permute-start | bytes 491528 | tf_op jit(solution)/shard_map/ppermute | solution.py:751
  57.2 10.0 %collective-permute-start.2 = (f32[2,64,128]{2,1,0:T(8,128)S(1)}, f32[2,64,128]{2,1,0:T(8,128)S(1)}, u32[]{:S(2)}, u32[]{:S(2)}) collective-permute-start(f32[2,64,128]{2,1,0:T(8,128)S(1)} %get-tuple-element.18), channel_id=1, source_target_pairs={{0,2},{1,3},{2,4},{3,5},{4,6},{5,7},{6,8},{7,9},{8,10},{9,11},{10,... | collective-permute-start | bytes 196616 | tf_op jit(solution)/shard_map/ppermute | solution.py:751
  57.4 9.8 %collective-permute-start.3 = (f32[2,64,128]{2,1,0:T(8,128)S(1)}, f32[2,64,128]{2,1,0:T(8,128)S(1)}, u32[]{:S(2)}, u32[]{:S(2)}) collective-permute-start(f32[2,64,128]{2,1,0:T(8,128)S(1)} %get-tuple-element.19), channel_id=1, source_target_pairs={{0,126},{1,127},{2,0},{3,1},{4,2},{5,3},{6,4},{7,5},{8,6},{9,7},{1... | collective-permute-start | bytes 196616 | tf_op jit(solution)/shard_map/ppermute | solution.py:751
  68.9 33.3 %collective-permute-start.8 = (bf16[1728,128]{1,0:T(8,128)(2,1)}, bf16[1728,128]{1,0:T(8,128)(2,1)S(1)}, u32[]{:S(2)}, u32[]{:S(2)}) collective-permute-start(bf16[1728,128]{1,0:T(8,128)(2,1)} %get-tuple-element.22), channel_id=1, source_target_pairs={{0,1},{1,2},{2,3},{3,4},{4,5},{5,6},{6,7},{7,8},{8,9},{9,10},{10,1... | collective-permute-start | bytes 1327112 | tf_op jit(solution)/shard_map/ppermute | solution.py:751
  69.8 32.4 %collective-permute-start.9 = (bf16[1728,128]{1,0:T(8,128)(2,1)S(1)}, bf16[1728,128]{1,0:T(8,128)(2,1)S(1)}, u32[]{:S(2)}, u32[]{:S(2)}) collective-permute-start(bf16[1728,128]{1,0:T(8,128)(2,1)S(1)} %get-tuple-element.23), channel_id=1, source_target_pairs={{0,127},{1,0},{2,1},{3,2},{4,3},{5,4},{6,5},{7,6},{8,7},{9,8},{10,... | collective-permute-start | bytes 1327112 | tf_op jit(solution)/shard_map/ppermute | solution.py:751
  90.1 5.0 %collective-permute-start.7 = (f32[8,24,128]{2,1,0:T(8,128)S(1)}, f32[8,24,128]{2,1,0:T(8,128)S(1)}, u32[]{:S(2)}, u32[]{:S(2)}) collective-permute-start(f32[8,24,128]{2,1,0:T(8,128)S(1)} %all_to_all.16.g2_ref), channel_id=1, source_target_pairs={{0,112},{1,113},{2,114},{3,115},{4,116},{5,117},{6,118},{7,119},{8... | collective-permute-start | bytes 294920 | tf_op jit(solution)/shard_map/ppermute | solution.py:751
  90.1 5.0 %collective-permute-start.6 = (f32[8,24,128]{2,1,0:T(8,128)S(1)}, f32[8,24,128]{2,1,0:T(8,128)S(1)}, u32[]{:S(2)}, u32[]{:S(2)}) collective-permute-start(f32[8,24,128]{2,1,0:T(8,128)S(1)} %all_to_all.16.g2_ref), channel_id=1, source_target_pairs={{0,120},{1,121},{2,122},{3,123},{4,124},{5,125},{6,126},{7,127},{8... | collective-permute-start | bytes 294920 | tf_op jit(solution)/shard_map/ppermute | solution.py:751
  91.1 7.0 %collective-permute-start.5 = (f32[8,24,128]{2,1,0:T(8,128)S(1)}, f32[8,24,128]{2,1,0:T(8,128)S(1)}, u32[]{:S(2)}, u32[]{:S(2)}) collective-permute-start(f32[8,24,128]{2,1,0:T(8,128)S(1)} %all_to_all.16.g2_ref), channel_id=1, source_target_pairs={{0,8},{1,9},{2,10},{3,11},{4,12},{5,13},{6,14},{7,15},{8,16},{9,17... | collective-permute-start | bytes 294920 | tf_op jit(solution)/shard_map/ppermute | solution.py:751
  95.1 7.1 %collective-permute-start.4 = (f32[8,24,128]{2,1,0:T(8,128)S(1)}, f32[8,24,128]{2,1,0:T(8,128)S(1)}, u32[]{:S(2)}, u32[]{:S(2)}) collective-permute-start(f32[8,24,128]{2,1,0:T(8,128)S(1)} %all_to_all.16.g2_ref), channel_id=1, source_target_pairs={{0,16},{1,17},{2,18},{3,19},{4,20},{5,21},{6,22},{7,23},{8,24},{9,... | collective-permute-start | bytes 294920 | tf_op jit(solution)/shard_map/ppermute | solution.py:751
  114.7 32.7 %copy-start.1 = (f32[128,3,256]{2,0,1:T(8,128)S(1)}, f32[128,3,256]{2,0,1:T(8,128)}, u32[]{:S(2)}) copy-start(f32[128,3,256]{2,0,1:T(8,128)} %param.5) | copy-start | bytes 1179652

commit v2 on v1

--- a/solution.py
+++ b/solution.py
@@ -9,7 +9,7 @@
 from jax.sharding import PartitionSpec as P
 
 AX = ("hi", "lo")
-LOCAL = 8
+LOCAL = 16
 BOX = 16
 CZ = 4
 HALF = CZ * BOX
@@ -542,12 +542,12 @@
 
 
 def up_kernel(
-    me_ref, meta_ref, lift_ref, g0_ref, g1_ref, g2_ref, g3_ref, g4_ref,
+    me_ref, meta_ref, lift_ref, g0_ref, g1_ref, g2_ref,
     pairs_ref, low_ref, own_ref, high_ref, vel_ref, pay_ref,
     window_ref, pool_ref, final_ref, lift1_ref, b1_ref, u1_ref, v1_ref, lift0_ref, u0_ref,
     v0_ref, ext_ref, halo_ref,
 ):
-    blocks = (g0_ref, g1_ref, g2_ref, g3_ref, g4_ref)
+    blocks = (g0_ref, g1_ref, g2_ref)
     coarse = coarse_part(me_ref[0], blocks, lift_ref, window_ref, pool_ref, final_ref)
     for c in range(3):
         spread = jnp.where(lanes(lambda r, l: r == 32 * c + (l & 63) // 2), 1.0, 0.0)
@@ -669,9 +669,9 @@
             shaped(own.shape, F32, False),
             shaped((slots, ROWS, 128), BF16),
         ),
-        [SMEM, SMEM] + [VMEM] * 10,
+        [SMEM, SMEM] + [VMEM] * 8,
         [
-            pltpu.VMEM((5 * LOCAL, 24, 128), F32),
+            pltpu.VMEM((3 * LOCAL, 24, 128), F32),
             pltpu.VMEM((480, 128), F32),
             pltpu.VMEM((6, 32, 128), F32),
             pltpu.VMEM((3, 320, 128), F32),
@@ -769,7 +769,7 @@
     pairs, share, rise, sink = middle_down(source, up, down, m1, p1, m2, p2)
     middle = exchanged(share, AX[1])
     low, high = moved(rise, 1), moved(sink, -1)
-    blocks = [middle if n == 0 else moved(middle, -LOCAL * n) for n in range(-2, 3)]
+    blocks = [middle if n == 0 else moved(middle, -LOCAL * n) for n in range(-1, 2)]
     velocity, picked = way_up(me, meta, lift, blocks, pairs, low, source, high, slots)
     out = read(dest, exchanged(picked), positions)
     return velocity, out.transpose(1, 0, 2)

time: 154 us -> 153 us (level)
  waiting for transfers between devices: 13.6 us -> 10.5 us
    ppermute x10 -> x8, waiting for transfers between devices: 13.6 us -> 10.5 us  [moved(): lax.ppermute(value, AX, [(i, (i + step) % size) for i in range(size)])]
    ppermute x10 -> x8, starting transfers between devices: 16.4 us -> 17.8 us  [moved(): lax.ppermute(value, AX, [(i, (i + step) % size) for i in range(size)])]
  transfers between devices with their start and end apart: 10 -> 8, of which waited for: 4 -> 3; matrix products, arithmetic and copies ran while one was open for 0% -> 0% of each run, Pallas kernels for 0% -> 0%
where the time goes in v2:
time: 153 us; the launch traced here: 152 us
  blocking collectives  83.6 us (55%)
  Pallas kernels  38.3 us (25%)
  starting transfers between devices  17.8 us (12%)
  waiting for transfers between devices  10.5 us (7%)
    all_to_all x3, blocking collectives, exchanged(): return lax.all_to_all(value, axes, split_axis=0, concat_axis=0, tiled=True)  83.6 us
    ppermute x8, starting transfers between devices, moved(): lax.ppermute(value, AX, [(i, (i + step) % size) for i in range(size)])  17.8 us
    pallas_call x1, Pallas kernels, way_up(): call(up_kernel, (shaped(own.shape, F32, False), shaped((slots, ROWS, 128)...  12.5 us
    ppermute x8, waiting for transfers between devices, moved(): lax.ppermute(value, AX, [(i, (i + step) % size) for i in range(size)])  10.5 us
    pallas_call x1, Pallas kernels, build(): call(build_kernel, shaped((slots, ROWS, 128), BF16), [SMEM, SMEM, VMEM, V...  9.87 us
    pallas_call x1, Pallas kernels, place(): call(place_kernel, (shaped(fluid.shape, F32), shaped((5, 64, 128), F32),...  7.91 us
    pallas_call x1, Pallas kernels, read(): call(read_kernel, shaped(positions.shape, F32, False), [SMEM, VMEM, VMEM]...  6.29 us
  transfers between devices with their start and end apart: 8, of which 3 were waited for; matrix products, arithmetic and copies ran while one was open for 0% of the time, Pallas kernels for 0%

profile of v2, /device:TPU:1, one launch (start us, length us, event | category | flops | bytes accessed | tf_op | source)
XLA Modules:
  0.0 152.4 jit_solution(18432383595231933413)
XLA Ops:
  0.6 9.9 %shard_map.68 = bf16[128,48,128]{2,1,0:T(8,128)(2,1)S(1)} custom-call(s32[1,128]{1,0:T(1,128)} %bitcast.10, s32[2,128]{1,0:T(2,128)} %bitcast.12, f32[3,128,256]{2,1,0:T(8,128)} %bitcast.6, f32[3,128,256]{2,1,0:T(8,128)} %bitcast.8, f32[4,3,128,128]{3,2,1,0:T(8,128)} %fluid_ref.3), custom_call_target="tpu_custom_call" | custom-call | tf_op jit(solution)/shard_map/pallas_call | solution.py:223
  10.5 0.0 copy-start
  10.5 36.1 %all_to_all.15.pay_ref = bf16[128,48,128]{2,1,0:T(8,128)(2,1)S(1)} all-to-all(bf16[128,48,128]{2,1,0:T(8,128)(2,1)S(1)} %shard_map.68), channel_id=1, replica_groups=mesh['hi'=8,'lo'=16] {'hi','lo'}, dimensions={0} | all-to-all | bytes 3145728 | tf_op jit(solution)/shard_map/all_to_all | solution.py:755
  46.7 1.1 slice.3
  47.8 0.2 convert_reduce_fusion
  48.0 0.1 reshape.16.meta_ref
  48.1 0.0 copy-done
  48.1 7.9 %shard_map.69 = (f32[4,3,128,128]{3,2,1,0:T(8,128)S(1)}, f32[5,64,128]{2,1,0:T(8,128)S(1)}, f32[5,64,128]{2,1,0:T(8,128)S(1)}, f32[2,64,128]{2,1,0:T(8,128)S(1)}...) custom-call(s32[1024]{0:T(1024)S(1)} %reshape.16.meta_ref, bf16[128,48,128]{2,1,0:T(8,128)(2,1)S(1)} %all_to_all.15.pay_ref, ...), custom_call_target="tpu_custom_call" | custom-call | tf_op jit(solution)/shard_map/pallas_call | solution.py:393
  56.0 1.2 collective-permute-start
  57.2 0.0 collective-permute-start.1
  57.2 0.2 collective-permute-start.2
  57.4 6.7 %collective-permute-start.3 = (f32[2,64,128]{2,1,0:T(8,128)S(1)}, f32[2,64,128]{2,1,0:T(8,128)S(1)}, u32[]{:S(2)}, u32[]{:S(2)}) collective-permute-start(f32[2,64,128]{2,1,0:T(8,128)S(1)} %get-tuple-element.19), channel_id=1, source_target_pairs={{0,126},{1,127},{2,0},{3,1},{4,2},{5,3},{6,4},{7,5},{8,6},{9,7},{1... | collective-permute-start | bytes 196616 | tf_op jit(solution)/shard_map/ppermute | solution.py:751
  64.1 3.1 %collective-permute-done.2.m2_ref = f32[2,64,128]{2,1,0:T(8,128)S(1)} collective-permute-done((f32[2,64,128]{2,1,0:T(8,128)S(1)}, f32[2,64,128]{2,1,0:T(8,128)S(1)}, u32[]{:S(2)}, u32[]{:S(2)}) %collective-permute-start.2) | collective-permute-done | bytes 65568 | tf_op jit(solution)/shard_map/ppermute | solution.py:751
  67.2 0.0 collective-permute-done.3.p2_ref
  67.2 0.0 collective-permute-done.m1_ref
  67.2 0.0 collective-permute-done.1.p1_ref
  67.2 1.7 %shard_map.70 = (f32[3,3,64,128]{3,2,1,0:T(8,128)S(1)}, f32[16,24,128]{2,1,0:T(8,128)S(1)}, bf16[1728,128]{1,0:T(8,128)(2,1)}, bf16[1728,128]{1,0:T(8,128)(2,1)S(1)}) custom-call(f32[4,3,128,128]{3,2,1,0:T(8,128)S(1)} %get-tuple-element.15.src_ref.own_ref, f32[5,64,128]{2,1,0:T(8,128)S(1)} %get-tuple-element.16.up_ref, ...), custom_call_target="tpu_custom_call" | custom-call | tf_op jit(solution)/shard_map/pallas_call | solution.py:488
  68.9 0.9 collective-permute-start.6
  69.8 5.8 %collective-permute-start.7 = (bf16[1728,128]{1,0:T(8,128)(2,1)S(1)}, bf16[1728,128]{1,0:T(8,128)(2,1)S(1)}, u32[]{:S(2)}, u32[]{:S(2)}) collective-permute-start(bf16[1728,128]{1,0:T(8,128)(2,1)S(1)} %get-tuple-element.23), channel_id=1, source_target_pairs={{0,127},{1,0},{2,1},{3,2},{4,3},{5,4},{6,5},{7,6},{8,7},{9,8},{10,... | collective-permute-start | bytes 1327112 | tf_op jit(solution)/shard_map/ppermute | solution.py:751
  75.6 17.0 %all_to_all.16.g1_ref = f32[16,24,128]{2,1,0:T(8,128)S(1)} all-to-all(f32[16,24,128]{2,1,0:T(8,128)S(1)} %get-tuple-element.20), channel_id=1, replica_groups=mesh['hi'=8,'lo'=16] {'lo'}, dimensions={0} | all-to-all | bytes 393216 | tf_op jit(solution)/shard_map/all_to_all | solution.py:755
  92.6 1.1 collective-permute-start.5
  93.7 1.9 %collective-permute-start.4 = (f32[16,24,128]{2,1,0:T(8,128)S(1)}, f32[16,24,128]{2,1,0:T(8,128)S(1)}, u32[]{:S(2)}, u32[]{:S(2)}) collective-permute-start(f32[16,24,128]{2,1,0:T(8,128)S(1)} %all_to_all.16.g1_ref), channel_id=1, source_target_pairs={{0,16},{1,17},{2,18},{3,19},{4,20},{5,21},{6,22},{7,23},{8,24},{9,... | collective-permute-start | bytes 589832 | tf_op jit(solution)/shard_map/ppermute | solution.py:751
  95.5 4.5 %collective-permute-done.5.g2_ref = f32[16,24,128]{2,1,0:T(8,128)S(1)} collective-permute-done((f32[16,24,128]{2,1,0:T(8,128)S(1)}, f32[16,24,128]{2,1,0:T(8,128)S(1)}, u32[]{:S(2)}, u32[]{:S(2)}) %collective-permute-start.5) | collective-permute-done | bytes 196640 | tf_op jit(solution)/shard_map/ppermute | solution.py:751
  100.1 2.9 %collective-permute-done.4.g0_ref = f32[16,24,128]{2,1,0:T(8,128)S(1)} collective-permute-done((f32[16,24,128]{2,1,0:T(8,128)S(1)}, f32[16,24,128]{2,1,0:T(8,128)S(1)}, u32[]{:S(2)}, u32[]{:S(2)}) %collective-permute-start.4) | collective-permute-done | bytes 196640 | tf_op jit(solution)/shard_map/ppermute | solution.py:751
  103.0 0.0 collective-permute-done.6.low_ref
  103.0 0.0 collective-permute-done.7.high_ref
  103.0 12.5 %shard_map.71 = (f32[4,3,128,128]{3,2,1,0:T(8,128)}, bf16[128,48,128]{2,1,0:T(8,128)(2,1)S(1)}) custom-call(s32[1]{0:T(128)} %bitcast.me_ref, s32[1024]{0:T(1024)S(1)} %reshape.16.meta_ref, f32[8,128]{1,0:T(8,128)S(1)} %get-tuple-element.14.lift_ref, f32[16,24,128]{2,1,0:T(8,128)S(1)} %collective-permute-done.4.g0_ref, ...), custom_call_target="tpu_custom_call" | custom-call | tf_op jit(solution)/shard_map/pallas_call | solution.py:666
  115.5 0.0 copy-start.1
  115.5 30.5 %all_to_all.17.pay_ref = bf16[128,48,128]{2,1,0:T(8,128)(2,1)S(1)} all-to-all(bf16[128,48,128]{2,1,0:T(8,128)(2,1)S(1)} %get-tuple-element.25), channel_id=1, replica_groups=mesh['hi'=8,'lo'=16] {'hi','lo'}, dimensions={0} | all-to-all | bytes 3145728 | tf_op jit(solution)/shard_map/all_to_all | solution.py:755
  146.1 0.0 copy-done.1
  146.1 6.3 %shard_map.72 = f32[3,128,256]{2,1,0:T(8,128)} custom-call(s32[1,128]{1,0:T(1,128)} %bitcast.11, bf16[128,48,128]{2,1,0:T(8,128)(2,1)S(1)} %all_to_all.17.pay_ref, f32[3,128,256]{2,1,0:T(8,128)S(1)} %bitcast.7), custom_call_target="tpu_custom_call" | custom-call | tf_op jit(solution)/shard_map/pallas_call | solution.py:737
Async XLA Ops:
  10.5 37.6 %copy-start = (f32[4,3,128,128]{3,2,1,0:T(8,128)S(1)}, f32[4,3,128,128]{3,2,1,0:T(8,128)}, u32[]{:S(2)}) copy-start(f32[4,3,128,128]{3,2,1,0:T(8,128)} %fluid_ref.3) | copy-start | bytes 2359300
  56.0 11.2 %collective-permute-start = (f32[5,64,128]{2,1,0:T(8,128)S(1)}, f32[5,64,128]{2,1,0:T(8,128)S(1)}, u32[]{:S(2)}, u32[]{:S(2)}) collective-permute-start(f32[5,64,128]{2,1,0:T(8,128)S(1)} %get-tuple-element.16.up_ref), channel_id=1, source_target_pairs={{0,1},{1,2},{2,3},{3,4},{4,5},{5,6},{6,7},{7,8},{8,9},{9,10},{10,1... | collective-permute-start | bytes 491528 | tf_op jit(solution)/shard_map/ppermute | solution.py:751
  57.2 10.0 %collective-permute-start.1 = (f32[5,64,128]{2,1,0:T(8,128)S(1)}, f32[5,64,128]{2,1,0:T(8,128)S(1)}, u32[]{:S(2)}, u32[]{:S(2)}) collective-permute-start(f32[5,64,128]{2,1,0:T(8,128)S(1)} %get-tuple-element.17.down_ref), channel_id=1, source_target_pairs={{0,127},{1,0},{2,1},{3,2},{4,3},{5,4},{6,5},{7,6},{8,7},{9,8},{10,... | collective-permute-start | bytes 491528 | tf_op jit(solution)/shard_map/ppermute | solution.py:751
  57.2 10.0 %collective-permute-start.2 = (f32[2,64,128]{2,1,0:T(8,128)S(1)}, f32[2,64,128]{2,1,0:T(8,128)S(1)}, u32[]{:S(2)}, u32[]{:S(2)}) collective-permute-start(f32[2,64,128]{2,1,0:T(8,128)S(1)} %get-tuple-element.18), channel_id=1, source_target_pairs={{0,2},{1,3},{2,4},{3,5},{4,6},{5,7},{6,8},{7,9},{8,10},{9,11},{10,... | collective-permute-start | bytes 196616 | tf_op jit(solution)/shard_map/ppermute | solution.py:751
  57.4 9.8 %collective-permute-start.3 = (f32[2,64,128]{2,1,0:T(8,128)S(1)}, f32[2,64,128]{2,1,0:T(8,128)S(1)}, u32[]{:S(2)}, u32[]{:S(2)}) collective-permute-start(f32[2,64,128]{2,1,0:T(8,128)S(1)} %get-tuple-element.19), channel_id=1, source_target_pairs={{0,126},{1,127},{2,0},{3,1},{4,2},{5,3},{6,4},{7,5},{8,6},{9,7},{1... | collective-permute-start | bytes 196616 | tf_op jit(solution)/shard_map/ppermute | solution.py:751
  68.9 34.1 %collective-permute-start.6 = (bf16[1728,128]{1,0:T(8,128)(2,1)}, bf16[1728,128]{1,0:T(8,128)(2,1)S(1)}, u32[]{:S(2)}, u32[]{:S(2)}) collective-permute-start(bf16[1728,128]{1,0:T(8,128)(2,1)} %get-tuple-element.22), channel_id=1, source_target_pairs={{0,1},{1,2},{2,3},{3,4},{4,5},{5,6},{6,7},{7,8},{8,9},{9,10},{10,1... | collective-permute-start | bytes 1327112 | tf_op jit(solution)/shard_map/ppermute | solution.py:751
  69.8 33.2 %collective-permute-start.7 = (bf16[1728,128]{1,0:T(8,128)(2,1)S(1)}, bf16[1728,128]{1,0:T(8,128)(2,1)S(1)}, u32[]{:S(2)}, u32[]{:S(2)}) collective-permute-start(bf16[1728,128]{1,0:T(8,128)(2,1)S(1)} %get-tuple-element.23), channel_id=1, source_target_pairs={{0,127},{1,0},{2,1},{3,2},{4,3},{5,4},{6,5},{7,6},{8,7},{9,8},{10,... | collective-permute-start | bytes 1327112 | tf_op jit(solution)/shard_map/ppermute | solution.py:751
  92.6 7.5 %collective-permute-start.5 = (f32[16,24,128]{2,1,0:T(8,128)S(1)}, f32[16,24,128]{2,1,0:T(8,128)S(1)}, u32[]{:S(2)}, u32[]{:S(2)}) collective-permute-start(f32[16,24,128]{2,1,0:T(8,128)S(1)} %all_to_all.16.g1_ref), channel_id=1, source_target_pairs={{0,112},{1,113},{2,114},{3,115},{4,116},{5,117},{6,118},{7,119},{8... | collective-permute-start | bytes 589832 | tf_op jit(solution)/shard_map/ppermute | solution.py:751
  93.7 9.3 %collective-permute-start.4 = (f32[16,24,128]{2,1,0:T(8,128)S(1)}, f32[16,24,128]{2,1,0:T(8,128)S(1)}, u32[]{:S(2)}, u32[]{:S(2)}) collective-permute-start(f32[16,24,128]{2,1,0:T(8,128)S(1)} %all_to_all.16.g1_ref), channel_id=1, source_target_pairs={{0,16},{1,17},{2,18},{3,19},{4,20},{5,21},{6,22},{7,23},{8,24},{9,... | collective-permute-start | bytes 589832 | tf_op jit(solution)/shard_map/ppermute | solution.py:751
  115.5 30.5 %copy-start.1 = (f32[128,3,256]{2,0,1:T(8,128)S(1)}, f32[128,3,256]{2,0,1:T(8,128)}, u32[]{:S(2)}) copy-start(f32[128,3,256]{2,0,1:T(8,128)} %param.5) | copy-start | bytes 1179652

commit v3 on v1

--- a/solution.py
+++ b/solution.py
@@ -385,8 +385,8 @@
         both = spill[0] + spill[1]
         ref[3] = both
         ref[4] = spill[2]
-        far_ref[0] = both
-        far_ref[1] = spill[2]
+        far_ref[0] = both.astype(BF16)
+        far_ref[1] = spill[2].astype(BF16)
 
 
 def place(meta, payload, fluid):
@@ -396,8 +396,8 @@
             shaped(fluid.shape, F32),
             shaped((5, 64, 128), F32),
             shaped((5, 64, 128), F32),
-            shaped((2, 64, 128), F32),
-            shaped((2, 64, 128), F32),
+            shaped((2, 64, 128), BF16),
+            shaped((2, 64, 128), BF16),
             shaped((8, 128), F32),
         ),
         [SMEM, VMEM, VMEM],
@@ -437,7 +437,7 @@
 
 
 def spilled(ref, c, first=0):
-    return both_layers(ref[first + c // 2])[c % 2]
+    return both_layers(ref[first + c // 2].astype(F32))[c % 2]
 
 
 U_ROW = 12 * 128
@@ -506,7 +506,7 @@
     parity = me % 2
     first = me % LOCAL - parity
     for n, ref in enumerate(blocks):
-        window_ref[LOCAL * n : LOCAL * n + LOCAL] = ref[...]
+        window_ref[LOCAL * n : LOCAL * n + LOCAL] = ref[...].astype(F32)
     b2 = jnp.stack([unpack_coarse(window_ref[first + t]) for t in range(34)])
     group = iota((1, 128), 1) // 32
     lift = jnp.zeros((1, 128), F32)
@@ -769,7 +769,10 @@
     pairs, share, rise, sink = middle_down(source, up, down, m1, p1, m2, p2)
     middle = exchanged(share, AX[1])
     low, high = moved(rise, 1), moved(sink, -1)
-    blocks = [middle if n == 0 else moved(middle, -LOCAL * n) for n in range(-2, 3)]
+    away = middle.astype(BF16)
+    above = [moved(middle, -LOCAL), moved(away, -2 * LOCAL)]
+    below = [moved(away, 2 * LOCAL), moved(middle, LOCAL)]
+    blocks = [*below, middle, *above]
     velocity, picked = way_up(me, meta, lift, blocks, pairs, low, source, high, slots)
     out = read(dest, exchanged(picked), positions)
     return velocity, out.transpose(1, 0, 2)

time: 154 us -> 152 us (0.987)
  transfers between devices with their start and end apart: 10 -> 10, of which waited for: 4 -> 3; matrix products, arithmetic and copies ran while one was open for 0% -> 0% of each run, Pallas kernels for 0% -> 0%
where the time goes in v3:
time: 152 us
  blocking collectives  82.5 us (54%)
  Pallas kernels  38.3 us (25%)
  starting transfers between devices  16.4 us (11%)
  waiting for transfers between devices  12.2 us (8%)
    all_to_all x3, blocking collectives, exchanged(): return lax.all_to_all(value, axes, split_axis=0, concat_axis=0, tiled=True)  82.5 us
    ppermute x10, starting transfers between devices, moved(): lax.ppermute(value, AX, [(i, (i + step) % size) for i in range(size)])  16.4 us
    pallas_call x1, Pallas kernels, way_up(): call(up_kernel, (shaped(own.shape, F32, False), shaped((slots, ROWS, 128)...  12.5 us
    ppermute x10, waiting for transfers between devices, moved(): lax.ppermute(value, AX, [(i, (i + step) % size) for i in range(size)])  12.2 us
    pallas_call x1, Pallas kernels, build(): call(build_kernel, shaped((slots, ROWS, 128), BF16), [SMEM, SMEM, VMEM, V...  9.87 us
    pallas_call x1, Pallas kernels, place(): call(place_kernel, (shaped(fluid.shape, F32), shaped((5, 64, 128), F32),...  7.91 us
    pallas_call x1, Pallas kernels, read(): call(read_kernel, shaped(positions.shape, F32, False), [SMEM, VMEM, VMEM]...  6.29 us
  transfers between devices with their start and end apart: 10, of which 3 were waited for; matrix products, arithmetic and copies ran while one was open for 0% of the time, Pallas kernels for 0%

profile of v3, /device:TPU:1, one launch (start us, length us, event | category | flops | bytes accessed | tf_op | source)
XLA Modules:
  0.0 151.6 jit_solution(17128832416633410437)
XLA Ops:
  0.6 9.9 %shard_map.68 = bf16[128,48,128]{2,1,0:T(8,128)(2,1)S(1)} custom-call(s32[1,128]{1,0:T(1,128)} %bitcast.10, s32[2,128]{1,0:T(2,128)} %bitcast.12, f32[3,128,256]{2,1,0:T(8,128)} %bitcast.6, f32[3,128,256]{2,1,0:T(8,128)} %bitcast.8, f32[4,3,128,128]{3,2,1,0:T(8,128)} %fluid_ref.3), custom_call_target="tpu_custom_call" | custom-call | tf_op jit(solution)/shard_map/pallas_call | solution.py:223
  10.5 0.0 copy-start
  10.5 36.1 %all_to_all.15.pay_ref = bf16[128,48,128]{2,1,0:T(8,128)(2,1)S(1)} all-to-all(bf16[128,48,128]{2,1,0:T(8,128)(2,1)S(1)} %shard_map.68), channel_id=1, replica_groups=mesh['hi'=16,'lo'=8] {'hi','lo'}, dimensions={0} | all-to-all | bytes 3145728 | tf_op jit(solution)/shard_map/all_to_all | solution.py:755
  46.7 1.1 slice.3
  47.8 0.2 convert_reduce_fusion
  48.0 0.1 reshape.16.meta_ref
  48.1 0.0 copy-done
  48.1 7.9 %shard_map.69 = (f32[4,3,128,128]{3,2,1,0:T(8,128)S(1)}, f32[5,64,128]{2,1,0:T(8,128)S(1)}, f32[5,64,128]{2,1,0:T(8,128)S(1)}, bf16[2,64,128]{2,1,0:T(8,128)(2,1...) custom-call(s32[1024]{0:T(1024)S(1)} %reshape.16.meta_ref, bf16[128,48,128]{2,1,0:T(8,128)(2,1)S(1)} %all_to_all.15.pay_ref, ...), custom_call_target="tpu_custom_call" | custom-call | tf_op jit(solution)/shard_map/pallas_call | solution.py:393
  56.0 1.2 collective-permute-start
  57.2 0.0 collective-permute-start.1
  57.2 0.2 collective-permute-start.2
  57.4 6.7 %collective-permute-start.3 = (bf16[2,64,128]{2,1,0:T(8,128)(2,1)S(1)}, bf16[2,64,128]{2,1,0:T(8,128)(2,1)S(1)}, u32[]{:S(2)}, u32[]{:S(2)}) collective-permute-start(bf16[2,64,128]{2,1,0:T(8,128)(2,1)S(1)} %get-tuple-element.19), channel_id=1, source_target_pairs={{0,126},{1,127},{2,0},{3,1},{4,2},{5,3},{6,4},{7,5},{8,6},{9,7},{1... | collective-permute-start | bytes 98312 | tf_op jit(solution)/shard_map/ppermute | solution.py:751
  64.1 2.8 %collective-permute-done.2.m2_ref = bf16[2,64,128]{2,1,0:T(8,128)(2,1)S(1)} collective-permute-done((bf16[2,64,128]{2,1,0:T(8,128)(2,1)S(1)}, bf16[2,64,128]{2,1,0:T(8,128)(2,1)S(1)}, u32[]{:S(2)}, u32[]{:S(2)}) %collective-permute-start.2) | collective-permute-done | bytes 32800 | tf_op jit(solution)/shard_map/ppermute | solution.py:751
  66.9 0.0 collective-permute-done.3.p2_ref
  66.9 0.0 collective-permute-done.m1_ref
  66.9 0.0 collective-permute-done.1.p1_ref
  66.9 1.7 %shard_map.70 = (f32[3,3,64,128]{3,2,1,0:T(8,128)S(1)}, f32[8,24,128]{2,1,0:T(8,128)S(1)}, bf16[1728,128]{1,0:T(8,128)(2,1)}, bf16[1728,128]{1,0:T(8,128)(2,1)S(1)}) custom-call(f32[4,3,128,128]{3,2,1,0:T(8,128)S(1)} %get-tuple-element.15.src_ref.own_ref, f32[5,64,128]{2,1,0:T(8,128)S(1)} %get-tuple-element.16.up_ref, ...), custom_call_target="tpu_custom_call" | custom-call | tf_op jit(solution)/shard_map/pallas_call | solution.py:488
  68.6 0.9 collective-permute-start.8
  69.4 5.8 %collective-permute-start.9 = (bf16[1728,128]{1,0:T(8,128)(2,1)S(1)}, bf16[1728,128]{1,0:T(8,128)(2,1)S(1)}, u32[]{:S(2)}, u32[]{:S(2)}) collective-permute-start(bf16[1728,128]{1,0:T(8,128)(2,1)S(1)} %get-tuple-element.23), channel_id=1, source_target_pairs={{0,127},{1,0},{2,1},{3,2},{4,3},{5,4},{6,5},{7,6},{8,7},{9,8},{10,... | collective-permute-start | bytes 1327112 | tf_op jit(solution)/shard_map/ppermute | solution.py:751
  75.3 14.5 %all_to_all.16.g2_ref = f32[8,24,128]{2,1,0:T(8,128)S(1)} all-to-all(f32[8,24,128]{2,1,0:T(8,128)S(1)} %get-tuple-element.20), channel_id=1, replica_groups=mesh['hi'=16,'lo'=8] {'lo'}, dimensions={0} | all-to-all | bytes 196608 | tf_op jit(solution)/shard_map/all_to_all | solution.py:755
  89.8 0.1 collective-permute-start.7
  89.9 1.1 collective-permute-start.6
  90.9 0.5 collective-permute-start.5
  91.4 2.9 %collective-permute-done.7.g4_ref = bf16[8,24,128]{2,1,0:T(8,128)(2,1)S(1)} collective-permute-done((bf16[8,24,128]{2,1,0:T(8,128)(2,1)S(1)}, bf16[8,24,128]{2,1,0:T(8,128)(2,1)S(1)}, u32[]{:S(2)}, u32[]{:S(2)}) %collective-permute-start.7) | collective-permute-done | bytes 49184 | tf_op jit(solution)/shard_map/ppermute | solution.py:751
  94.3 0.0 collective-permute-start.4
  94.3 6.6 %collective-permute-done.4.g0_ref = bf16[8,24,128]{2,1,0:T(8,128)(2,1)S(1)} collective-permute-done((bf16[8,24,128]{2,1,0:T(8,128)(2,1)S(1)}, bf16[8,24,128]{2,1,0:T(8,128)(2,1)S(1)}, u32[]{:S(2)}, u32[]{:S(2)}) %collective-permute-start.4) | collective-permute-done | bytes 49184 | tf_op jit(solution)/shard_map/ppermute | solution.py:751
  100.9 0.0 collective-permute-done.6.g3_ref
  100.9 0.0 collective-permute-done.5.g1_ref
  100.9 0.0 collective-permute-done.8.low_ref
  100.9 0.0 collective-permute-done.9.high_ref
  100.9 12.5 %shard_map.71 = (f32[4,3,128,128]{3,2,1,0:T(8,128)}, bf16[128,48,128]{2,1,0:T(8,128)(2,1)S(1)}) custom-call(s32[1]{0:T(128)} %bitcast.me_ref, s32[1024]{0:T(1024)S(1)} %reshape.16.meta_ref, f32[8,128]{1,0:T(8,128)S(1)} %get-tuple-element.14.lift_ref, bf16[8,24,128]{2,1,0:T(8,128)(2,1)S(1)} %collective-permute-done.4.g0_ref, ...), custom_call_target="tpu_custom_call" | custom-call | tf_op jit(solution)/shard_map/pallas_call | solution.py:666
  113.4 0.0 copy-start.1
  113.4 31.8 %all_to_all.17.pay_ref = bf16[128,48,128]{2,1,0:T(8,128)(2,1)S(1)} all-to-all(bf16[128,48,128]{2,1,0:T(8,128)(2,1)S(1)} %get-tuple-element.25), channel_id=1, replica_groups=mesh['hi'=16,'lo'=8] {'hi','lo'}, dimensions={0} | all-to-all | bytes 3145728 | tf_op jit(solution)/shard_map/all_to_all | solution.py:755
  145.3 0.0 copy-done.1
  145.3 6.3 %shard_map.72 = f32[3,128,256]{2,1,0:T(8,128)} custom-call(s32[1,128]{1,0:T(1,128)} %bitcast.11, bf16[128,48,128]{2,1,0:T(8,128)(2,1)S(1)} %all_to_all.17.pay_ref, f32[3,128,256]{2,1,0:T(8,128)S(1)} %bitcast.7), custom_call_target="tpu_custom_call" | custom-call | tf_op jit(solution)/shard_map/pallas_call | solution.py:737
  (1 shorter events, 0.0 us)
Async XLA Ops:
  10.5 37.6 %copy-start = (f32[4,3,128,128]{3,2,1,0:T(8,128)S(1)}, f32[4,3,128,128]{3,2,1,0:T(8,128)}, u32[]{:S(2)}) copy-start(f32[4,3,128,128]{3,2,1,0:T(8,128)} %fluid_ref.3) | copy-start | bytes 2359300
  56.0 10.9 %collective-permute-start = (f32[5,64,128]{2,1,0:T(8,128)S(1)}, f32[5,64,128]{2,1,0:T(8,128)S(1)}, u32[]{:S(2)}, u32[]{:S(2)}) collective-permute-start(f32[5,64,128]{2,1,0:T(8,128)S(1)} %get-tuple-element.16.up_ref), channel_id=1, source_target_pairs={{0,1},{1,2},{2,3},{3,4},{4,5},{5,6},{6,7},{7,8},{8,9},{9,10},{10,1... | collective-permute-start | bytes 491528 | tf_op jit(solution)/shard_map/ppermute | solution.py:751
  57.2 9.7 %collective-permute-start.1 = (f32[5,64,128]{2,1,0:T(8,128)S(1)}, f32[5,64,128]{2,1,0:T(8,128)S(1)}, u32[]{:S(2)}, u32[]{:S(2)}) collective-permute-start(f32[5,64,128]{2,1,0:T(8,128)S(1)} %get-tuple-element.17.down_ref), channel_id=1, source_target_pairs={{0,127},{1,0},{2,1},{3,2},{4,3},{5,4},{6,5},{7,6},{8,7},{9,8},{10,... | collective-permute-start | bytes 491528 | tf_op jit(solution)/shard_map/ppermute | solution.py:751
  57.2 9.6 %collective-permute-start.2 = (bf16[2,64,128]{2,1,0:T(8,128)(2,1)S(1)}, bf16[2,64,128]{2,1,0:T(8,128)(2,1)S(1)}, u32[]{:S(2)}, u32[]{:S(2)}) collective-permute-start(bf16[2,64,128]{2,1,0:T(8,128)(2,1)S(1)} %get-tuple-element.18), channel_id=1, source_target_pairs={{0,2},{1,3},{2,4},{3,5},{4,6},{5,7},{6,8},{7,9},{8,10},{9,11},{10,... | collective-permute-start | bytes 98312 | tf_op jit(solution)/shard_map/ppermute | solution.py:751
  57.4 9.5 %collective-permute-start.3 = (bf16[2,64,128]{2,1,0:T(8,128)(2,1)S(1)}, bf16[2,64,128]{2,1,0:T(8,128)(2,1)S(1)}, u32[]{:S(2)}, u32[]{:S(2)}) collective-permute-start(bf16[2,64,128]{2,1,0:T(8,128)(2,1)S(1)} %get-tuple-element.19), channel_id=1, source_target_pairs={{0,126},{1,127},{2,0},{3,1},{4,2},{5,3},{6,4},{7,5},{8,6},{9,7},{1... | collective-permute-start | bytes 98312 | tf_op jit(solution)/shard_map/ppermute | solution.py:751
  68.6 32.3 %collective-permute-start.8 = (bf16[1728,128]{1,0:T(8,128)(2,1)}, bf16[1728,128]{1,0:T(8,128)(2,1)S(1)}, u32[]{:S(2)}, u32[]{:S(2)}) collective-permute-start(bf16[1728,128]{1,0:T(8,128)(2,1)} %get-tuple-element.22), channel_id=1, source_target_pairs={{0,1},{1,2},{2,3},{3,4},{4,5},{5,6},{6,7},{7,8},{8,9},{9,10},{10,1... | collective-permute-start | bytes 1327112 | tf_op jit(solution)/shard_map/ppermute | solution.py:751
  69.4 31.4 %collective-permute-start.9 = (bf16[1728,128]{1,0:T(8,128)(2,1)S(1)}, bf16[1728,128]{1,0:T(8,128)(2,1)S(1)}, u32[]{:S(2)}, u32[]{:S(2)}) collective-permute-start(bf16[1728,128]{1,0:T(8,128)(2,1)S(1)} %get-tuple-element.23), channel_id=1, source_target_pairs={{0,127},{1,0},{2,1},{3,2},{4,3},{5,4},{6,5},{7,6},{8,7},{9,8},{10,... | collective-permute-start | bytes 1327112 | tf_op jit(solution)/shard_map/ppermute | solution.py:751
  89.8 4.5 %collective-permute-start.7 = (bf16[8,24,128]{2,1,0:T(8,128)(2,1)S(1)}, bf16[8,24,128]{2,1,0:T(8,128)(2,1)S(1)}, u32[]{:S(2)}, u32[]{:S(2)}) collective-permute-start(bf16[8,24,128]{2,1,0:T(8,128)(2,1)S(1)} %convert_element_type.4), channel_id=1, source_target_pairs={{0,112},{1,113},{2,114},{3,115},{4,116},{5,117},{6,118},{7,119},{8... | collective-permute-start | bytes 147464 | tf_op jit(solution)/shard_map/ppermute | solution.py:751
  89.9 11.0 %collective-permute-start.6 = (f32[8,24,128]{2,1,0:T(8,128)S(1)}, f32[8,24,128]{2,1,0:T(8,128)S(1)}, u32[]{:S(2)}, u32[]{:S(2)}) collective-permute-start(f32[8,24,128]{2,1,0:T(8,128)S(1)} %all_to_all.16.g2_ref), channel_id=1, source_target_pairs={{0,120},{1,121},{2,122},{3,123},{4,124},{5,125},{6,126},{7,127},{8... | collective-permute-start | bytes 294920 | tf_op jit(solution)/shard_map/ppermute | solution.py:751
  90.9 9.9 %collective-permute-start.5 = (f32[8,24,128]{2,1,0:T(8,128)S(1)}, f32[8,24,128]{2,1,0:T(8,128)S(1)}, u32[]{:S(2)}, u32[]{:S(2)}) collective-permute-start(f32[8,24,128]{2,1,0:T(8,128)S(1)} %all_to_all.16.g2_ref), channel_id=1, source_target_pairs={{0,8},{1,9},{2,10},{3,11},{4,12},{5,13},{6,14},{7,15},{8,16},{9,17... | collective-permute-start | bytes 294920 | tf_op jit(solution)/shard_map/ppermute | solution.py:751
  94.3 6.6 %collective-permute-start.4 = (bf16[8,24,128]{2,1,0:T(8,128)(2,1)S(1)}, bf16[8,24,128]{2,1,0:T(8,128)(2,1)S(1)}, u32[]{:S(2)}, u32[]{:S(2)}) collective-permute-start(bf16[8,24,128]{2,1,0:T(8,128)(2,1)S(1)} %convert_element_type.4), channel_id=1, source_target_pairs={{0,16},{1,17},{2,18},{3,19},{4,20},{5,21},{6,22},{7,23},{8,24},{9,... | collective-permute-start | bytes 147464 | tf_op jit(solution)/shard_map/ppermute | solution.py:751
  113.4 31.8 %copy-start.1 = (f32[128,3,256]{2,0,1:T(8,128)S(1)}, f32[128,3,256]{2,0,1:T(8,128)}, u32[]{:S(2)}) copy-start(f32[128,3,256]{2,0,1:T(8,128)} %param.5) | copy-start | bytes 1179652

commit v4 on v3

--- a/solution.py
+++ b/solution.py
@@ -140,7 +140,7 @@
 ):
     slots = out_ref.shape[0]
     blocks = pos_ref.shape[1]
-    group = together(blocks, 16)
+    group = together(blocks, 32)
 
     def clear(t, carry):
         count_ref[t] = 0
@@ -227,7 +227,7 @@
         [
             pltpu.VMEM((slots, ROWS, 128), F32),
             pltpu.SMEM((slots,), jnp.int32),
-            pltpu.VMEM((9, together(positions.shape[1], 16), 256), F32),
+            pltpu.VMEM((9, together(positions.shape[1], 32), 256), F32),
         ],
     )(*map(far, (dest, base, positions, forces, fluid)))
 
@@ -315,7 +315,7 @@
                 )
                 grid_ref[kc, pl.ds(row + 16, 8), :] += jnp.where(early, second, 0.0)
 
-    group = together(slots, 8)
+    group = together(slots, 16)
 
     def several(step, carry):
         found = []
@@ -637,7 +637,7 @@
             values.append(line)
         return (8 - shift) & 7, values
 
-    group = together(pay_ref.shape[0], 8)
+    group = together(pay_ref.shape[0], 16)
 
     def several(step, carry):
         found = []
@@ -698,7 +698,7 @@
     lax.fori_loop(0, slots, widen, 0, unroll=4)
     lane = iota((8, 128), 1)
 
-    group = together(pos_ref.shape[1], 16)
+    group = together(pos_ref.shape[1], 32)
 
     def one(first, n, target, order):
         block = first + n
@@ -741,7 +741,7 @@
         [
             pltpu.VMEM((slots, ROWS, 128), F32),
             pltpu.SMEM((slots,), jnp.int32),
-            pltpu.VMEM((9, together(positions.shape[1], 16), 256), F32),
+            pltpu.VMEM((9, together(positions.shape[1], 32), 256), F32),
         ],
     )(far(dest), near(payload), near(positions))
 

time: 152 us -> 150 us (0.987)
  Pallas kernels: 38.3 us -> 36.3 us
where the time goes in v4:
time: 150 us
  blocking collectives  82.5 us (55%)
  Pallas kernels  36.3 us (24%)
  starting transfers between devices  16.4 us (11%)
  waiting for transfers between devices  12.2 us (8%)
    all_to_all x3, blocking collectives, exchanged(): return lax.all_to_all(value, axes, split_axis=0, concat_axis=0, tiled=True)  82.5 us
    ppermute x10, starting transfers between devices, moved(): lax.ppermute(value, AX, [(i, (i + step) % size) for i in range(size)])  16.4 us
    ppermute x10, waiting for transfers between devices, moved(): lax.ppermute(value, AX, [(i, (i + step) % size) for i in range(size)])  12.2 us
    pallas_call x1, Pallas kernels, way_up(): call(up_kernel, (shaped(own.shape, F32, False), shaped((slots, ROWS, 128)...  11.9 us
    pallas_call x1, Pallas kernels, build(): call(build_kernel, shaped((slots, ROWS, 128), BF16), [SMEM, SMEM, VMEM, V...  8.96 us
    pallas_call x1, Pallas kernels, place(): call(place_kernel, (shaped(fluid.shape, F32), shaped((5, 64, 128), F32),...  7.59 us
    pallas_call x1, Pallas kernels, read(): call(read_kernel, shaped(positions.shape, F32, False), [SMEM, VMEM, VMEM]...  6.15 us
  transfers between devices with their start and end apart: 10, of which 3 were waited for; matrix products, arithmetic and copies ran while one was open for 0% of the time, Pallas kernels for 0%

profile of v4, /device:TPU:1, one launch (start us, length us, event | category | flops | bytes accessed | tf_op | source)
XLA Modules:
  0.0 149.6 jit_solution(306399712156659955)
XLA Ops:
  0.6 9.0 %shard_map.68 = bf16[128,48,128]{2,1,0:T(8,128)(2,1)S(1)} custom-call(s32[1,128]{1,0:T(1,128)} %bitcast.10, s32[2,128]{1,0:T(2,128)} %bitcast.12, f32[3,128,256]{2,1,0:T(8,128)} %bitcast.6, f32[3,128,256]{2,1,0:T(8,128)} %bitcast.8, f32[4,3,128,128]{3,2,1,0:T(8,128)} %fluid_ref.3), custom_call_target="tpu_custom_call" | custom-call | tf_op jit(solution)/shard_map/pallas_call | solution.py:223
  9.6 0.0 copy-start
  9.6 36.1 %all_to_all.15.pay_ref = bf16[128,48,128]{2,1,0:T(8,128)(2,1)S(1)} all-to-all(bf16[128,48,128]{2,1,0:T(8,128)(2,1)S(1)} %shard_map.68), channel_id=1, replica_groups=mesh['hi'=16,'lo'=8] {'hi','lo'}, dimensions={0} | all-to-all | bytes 3145728 | tf_op jit(solution)/shard_map/all_to_all | solution.py:755
  45.7 1.1 slice.3
  46.9 0.2 convert_reduce_fusion
  47.1 0.1 reshape.16.meta_ref
  47.2 0.0 copy-done
  47.2 7.6 %shard_map.69 = (f32[4,3,128,128]{3,2,1,0:T(8,128)S(1)}, f32[5,64,128]{2,1,0:T(8,128)S(1)}, f32[5,64,128]{2,1,0:T(8,128)S(1)}, bf16[2,64,128]{2,1,0:T(8,128)(2,1...) custom-call(s32[1024]{0:T(1024)S(1)} %reshape.16.meta_ref, bf16[128,48,128]{2,1,0:T(8,128)(2,1)S(1)} %all_to_all.15.pay_ref, ...), custom_call_target="tpu_custom_call" | custom-call | tf_op jit(solution)/shard_map/pallas_call | solution.py:393
  54.8 1.2 collective-permute-start
  56.0 0.0 collective-permute-start.1
  56.0 0.2 collective-permute-start.2
  56.2 6.7 %collective-permute-start.3 = (bf16[2,64,128]{2,1,0:T(8,128)(2,1)S(1)}, bf16[2,64,128]{2,1,0:T(8,128)(2,1)S(1)}, u32[]{:S(2)}, u32[]{:S(2)}) collective-permute-start(bf16[2,64,128]{2,1,0:T(8,128)(2,1)S(1)} %get-tuple-element.19), channel_id=1, source_target_pairs={{0,126},{1,127},{2,0},{3,1},{4,2},{5,3},{6,4},{7,5},{8,6},{9,7},{1... | collective-permute-start | bytes 98312 | tf_op jit(solution)/shard_map/ppermute | solution.py:751
  62.9 2.8 %collective-permute-done.2.m2_ref = bf16[2,64,128]{2,1,0:T(8,128)(2,1)S(1)} collective-permute-done((bf16[2,64,128]{2,1,0:T(8,128)(2,1)S(1)}, bf16[2,64,128]{2,1,0:T(8,128)(2,1)S(1)}, u32[]{:S(2)}, u32[]{:S(2)}) %collective-permute-start.2) | collective-permute-done | bytes 32800 | tf_op jit(solution)/shard_map/ppermute | solution.py:751
  65.6 0.0 collective-permute-done.3.p2_ref
  65.6 0.0 collective-permute-done.m1_ref
  65.6 0.0 collective-permute-done.1.p1_ref
  65.6 1.7 %shard_map.70 = (f32[3,3,64,128]{3,2,1,0:T(8,128)S(1)}, f32[8,24,128]{2,1,0:T(8,128)S(1)}, bf16[1728,128]{1,0:T(8,128)(2,1)}, bf16[1728,128]{1,0:T(8,128)(2,1)S(1)}) custom-call(f32[4,3,128,128]{3,2,1,0:T(8,128)S(1)} %get-tuple-element.15.src_ref.own_ref, f32[5,64,128]{2,1,0:T(8,128)S(1)} %get-tuple-element.16.up_ref, ...), custom_call_target="tpu_custom_call" | custom-call | tf_op jit(solution)/shard_map/pallas_call | solution.py:488
  67.3 0.9 collective-permute-start.8
  68.2 5.8 %collective-permute-start.9 = (bf16[1728,128]{1,0:T(8,128)(2,1)S(1)}, bf16[1728,128]{1,0:T(8,128)(2,1)S(1)}, u32[]{:S(2)}, u32[]{:S(2)}) collective-permute-start(bf16[1728,128]{1,0:T(8,128)(2,1)S(1)} %get-tuple-element.23), channel_id=1, source_target_pairs={{0,127},{1,0},{2,1},{3,2},{4,3},{5,4},{6,5},{7,6},{8,7},{9,8},{10,... | collective-permute-start | bytes 1327112 | tf_op jit(solution)/shard_map/ppermute | solution.py:751
  74.0 14.5 %all_to_all.16.g2_ref = f32[8,24,128]{2,1,0:T(8,128)S(1)} all-to-all(f32[8,24,128]{2,1,0:T(8,128)S(1)} %get-tuple-element.20), channel_id=1, replica_groups=mesh['hi'=16,'lo'=8] {'lo'}, dimensions={0} | all-to-all | bytes 196608 | tf_op jit(solution)/shard_map/all_to_all | solution.py:755
  88.5 0.1 collective-permute-start.7
  88.6 1.1 collective-permute-start.6
  89.7 0.5 collective-permute-start.5
  90.2 2.9 %collective-permute-done.7.g4_ref = bf16[8,24,128]{2,1,0:T(8,128)(2,1)S(1)} collective-permute-done((bf16[8,24,128]{2,1,0:T(8,128)(2,1)S(1)}, bf16[8,24,128]{2,1,0:T(8,128)(2,1)S(1)}, u32[]{:S(2)}, u32[]{:S(2)}) %collective-permute-start.7) | collective-permute-done | bytes 49184 | tf_op jit(solution)/shard_map/ppermute | solution.py:751
  93.1 0.0 collective-permute-start.4
  93.1 6.6 %collective-permute-done.4.g0_ref = bf16[8,24,128]{2,1,0:T(8,128)(2,1)S(1)} collective-permute-done((bf16[8,24,128]{2,1,0:T(8,128)(2,1)S(1)}, bf16[8,24,128]{2,1,0:T(8,128)(2,1)S(1)}, u32[]{:S(2)}, u32[]{:S(2)}) %collective-permute-start.4) | collective-permute-done | bytes 49184 | tf_op jit(solution)/shard_map/ppermute | solution.py:751
  99.6 0.0 collective-permute-done.6.g3_ref
  99.6 0.0 collective-permute-done.5.g1_ref
  99.6 0.0 collective-permute-done.8.low_ref
  99.6 0.0 collective-permute-done.9.high_ref
  99.6 11.9 %shard_map.71 = (f32[4,3,128,128]{3,2,1,0:T(8,128)}, bf16[128,48,128]{2,1,0:T(8,128)(2,1)S(1)}) custom-call(s32[1]{0:T(128)} %bitcast.me_ref, s32[1024]{0:T(1024)S(1)} %reshape.16.meta_ref, f32[8,128]{1,0:T(8,128)S(1)} %get-tuple-element.14.lift_ref, bf16[8,24,128]{2,1,0:T(8,128)(2,1)S(1)} %collective-permute-done.4.g0_ref, ...), custom_call_target="tpu_custom_call" | custom-call | tf_op jit(solution)/shard_map/pallas_call | solution.py:666
  111.6 0.0 copy-start.1
  111.6 31.8 %all_to_all.17.pay_ref = bf16[128,48,128]{2,1,0:T(8,128)(2,1)S(1)} all-to-all(bf16[128,48,128]{2,1,0:T(8,128)(2,1)S(1)} %get-tuple-element.25), channel_id=1, replica_groups=mesh['hi'=16,'lo'=8] {'hi','lo'}, dimensions={0} | all-to-all | bytes 3145728 | tf_op jit(solution)/shard_map/all_to_all | solution.py:755
  143.4 0.0 copy-done.1
  143.4 6.2 %shard_map.72 = f32[3,128,256]{2,1,0:T(8,128)} custom-call(s32[1,128]{1,0:T(1,128)} %bitcast.11, bf16[128,48,128]{2,1,0:T(8,128)(2,1)S(1)} %all_to_all.17.pay_ref, f32[3,128,256]{2,1,0:T(8,128)S(1)} %bitcast.7), custom_call_target="tpu_custom_call" | custom-call | tf_op jit(solution)/shard_map/pallas_call | solution.py:737
  (1 shorter events, 0.0 us)
Async XLA Ops:
  9.6 37.6 %copy-start = (f32[4,3,128,128]{3,2,1,0:T(8,128)S(1)}, f32[4,3,128,128]{3,2,1,0:T(8,128)}, u32[]{:S(2)}) copy-start(f32[4,3,128,128]{3,2,1,0:T(8,128)} %fluid_ref.3) | copy-start | bytes 2359300
  54.8 10.9 %collective-permute-start = (f32[5,64,128]{2,1,0:T(8,128)S(1)}, f32[5,64,128]{2,1,0:T(8,128)S(1)}, u32[]{:S(2)}, u32[]{:S(2)}) collective-permute-start(f32[5,64,128]{2,1,0:T(8,128)S(1)} %get-tuple-element.16.up_ref), channel_id=1, source_target_pairs={{0,1},{1,2},{2,3},{3,4},{4,5},{5,6},{6,7},{7,8},{8,9},{9,10},{10,1... | collective-permute-start | bytes 491528 | tf_op jit(solution)/shard_map/ppermute | solution.py:751
  56.0 9.7 %collective-permute-start.1 = (f32[5,64,128]{2,1,0:T(8,128)S(1)}, f32[5,64,128]{2,1,0:T(8,128)S(1)}, u32[]{:S(2)}, u32[]{:S(2)}) collective-permute-start(f32[5,64,128]{2,1,0:T(8,128)S(1)} %get-tuple-element.17.down_ref), channel_id=1, source_target_pairs={{0,127},{1,0},{2,1},{3,2},{4,3},{5,4},{6,5},{7,6},{8,7},{9,8},{10,... | collective-permute-start | bytes 491528 | tf_op jit(solution)/shard_map/ppermute | solution.py:751
  56.0 9.6 %collective-permute-start.2 = (bf16[2,64,128]{2,1,0:T(8,128)(2,1)S(1)}, bf16[2,64,128]{2,1,0:T(8,128)(2,1)S(1)}, u32[]{:S(2)}, u32[]{:S(2)}) collective-permute-start(bf16[2,64,128]{2,1,0:T(8,128)(2,1)S(1)} %get-tuple-element.18), channel_id=1, source_target_pairs={{0,2},{1,3},{2,4},{3,5},{4,6},{5,7},{6,8},{7,9},{8,10},{9,11},{10,... | collective-permute-start | bytes 98312 | tf_op jit(solution)/shard_map/ppermute | solution.py:751
  56.2 9.5 %collective-permute-start.3 = (bf16[2,64,128]{2,1,0:T(8,128)(2,1)S(1)}, bf16[2,64,128]{2,1,0:T(8,128)(2,1)S(1)}, u32[]{:S(2)}, u32[]{:S(2)}) collective-permute-start(bf16[2,64,128]{2,1,0:T(8,128)(2,1)S(1)} %get-tuple-element.19), channel_id=1, source_target_pairs={{0,126},{1,127},{2,0},{3,1},{4,2},{5,3},{6,4},{7,5},{8,6},{9,7},{1... | collective-permute-start | bytes 98312 | tf_op jit(solution)/shard_map/ppermute | solution.py:751
  67.3 32.3 %collective-permute-start.8 = (bf16[1728,128]{1,0:T(8,128)(2,1)}, bf16[1728,128]{1,0:T(8,128)(2,1)S(1)}, u32[]{:S(2)}, u32[]{:S(2)}) collective-permute-start(bf16[1728,128]{1,0:T(8,128)(2,1)} %get-tuple-element.22), channel_id=1, source_target_pairs={{0,1},{1,2},{2,3},{3,4},{4,5},{5,6},{6,7},{7,8},{8,9},{9,10},{10,1... | collective-permute-start | bytes 1327112 | tf_op jit(solution)/shard_map/ppermute | solution.py:751
  68.2 31.4 %collective-permute-start.9 = (bf16[1728,128]{1,0:T(8,128)(2,1)S(1)}, bf16[1728,128]{1,0:T(8,128)(2,1)S(1)}, u32[]{:S(2)}, u32[]{:S(2)}) collective-permute-start(bf16[1728,128]{1,0:T(8,128)(2,1)S(1)} %get-tuple-element.23), channel_id=1, source_target_pairs={{0,127},{1,0},{2,1},{3,2},{4,3},{5,4},{6,5},{7,6},{8,7},{9,8},{10,... | collective-permute-start | bytes 1327112 | tf_op jit(solution)/shard_map/ppermute | solution.py:751
  88.5 4.5 %collective-permute-start.7 = (bf16[8,24,128]{2,1,0:T(8,128)(2,1)S(1)}, bf16[8,24,128]{2,1,0:T(8,128)(2,1)S(1)}, u32[]{:S(2)}, u32[]{:S(2)}) collective-permute-start(bf16[8,24,128]{2,1,0:T(8,128)(2,1)S(1)} %convert_element_type.4), channel_id=1, source_target_pairs={{0,112},{1,113},{2,114},{3,115},{4,116},{5,117},{6,118},{7,119},{8... | collective-permute-start | bytes 147464 | tf_op jit(solution)/shard_map/ppermute | solution.py:751
  88.6 11.0 %collective-permute-start.6 = (f32[8,24,128]{2,1,0:T(8,128)S(1)}, f32[8,24,128]{2,1,0:T(8,128)S(1)}, u32[]{:S(2)}, u32[]{:S(2)}) collective-permute-start(f32[8,24,128]{2,1,0:T(8,128)S(1)} %all_to_all.16.g2_ref), channel_id=1, source_target_pairs={{0,120},{1,121},{2,122},{3,123},{4,124},{5,125},{6,126},{7,127},{8... | collective-permute-start | bytes 294920 | tf_op jit(solution)/shard_map/ppermute | solution.py:751
  89.7 9.9 %collective-permute-start.5 = (f32[8,24,128]{2,1,0:T(8,128)S(1)}, f32[8,24,128]{2,1,0:T(8,128)S(1)}, u32[]{:S(2)}, u32[]{:S(2)}) collective-permute-start(f32[8,24,128]{2,1,0:T(8,128)S(1)} %all_to_all.16.g2_ref), channel_id=1, source_target_pairs={{0,8},{1,9},{2,10},{3,11},{4,12},{5,13},{6,14},{7,15},{8,16},{9,17... | collective-permute-start | bytes 294920 | tf_op jit(solution)/shard_map/ppermute | solution.py:751
  93.1 6.6 %collective-permute-start.4 = (bf16[8,24,128]{2,1,0:T(8,128)(2,1)S(1)}, bf16[8,24,128]{2,1,0:T(8,128)(2,1)S(1)}, u32[]{:S(2)}, u32[]{:S(2)}) collective-permute-start(bf16[8,24,128]{2,1,0:T(8,128)(2,1)S(1)} %convert_element_type.4), channel_id=1, source_target_pairs={{0,16},{1,17},{2,18},{3,19},{4,20},{5,21},{6,22},{7,23},{8,24},{9,... | collective-permute-start | bytes 147464 | tf_op jit(solution)/shard_map/ppermute | solution.py:751
  111.6 31.8 %copy-start.1 = (f32[128,3,256]{2,0,1:T(8,128)S(1)}, f32[128,3,256]{2,0,1:T(8,128)}, u32[]{:S(2)}) copy-start(f32[128,3,256]{2,0,1:T(8,128)} %param.5) | copy-start | bytes 1179652

commit v5 on v4

--- a/solution.py
+++ b/solution.py
@@ -140,7 +140,7 @@
 ):
     slots = out_ref.shape[0]
     blocks = pos_ref.shape[1]
-    group = together(blocks, 32)
+    group = together(blocks, 64)
 
     def clear(t, carry):
         count_ref[t] = 0
@@ -227,7 +227,7 @@
         [
             pltpu.VMEM((slots, ROWS, 128), F32),
             pltpu.SMEM((slots,), jnp.int32),
-            pltpu.VMEM((9, together(positions.shape[1], 32), 256), F32),
+            pltpu.VMEM((9, together(positions.shape[1], 64), 256), F32),
         ],
     )(*map(far, (dest, base, positions, forces, fluid)))
 
@@ -315,7 +315,7 @@
                 )
                 grid_ref[kc, pl.ds(row + 16, 8), :] += jnp.where(early, second, 0.0)
 
-    group = together(slots, 16)
+    group = together(slots, 32)
 
     def several(step, carry):
         found = []
@@ -637,7 +637,7 @@
             values.append(line)
         return (8 - shift) & 7, values
 
-    group = together(pay_ref.shape[0], 16)
+    group = together(pay_ref.shape[0], 32)
 
     def several(step, carry):
         found = []

time: 150 us -> 149 us (level)
  no operation moved by 1% of the time
where the time goes in v5:
time: 149 us
  blocking collectives  82.5 us (55%)
  Pallas kernels  35.4 us (24%)
  starting transfers between devices  16.4 us (11%)
  waiting for transfers between devices  12.2 us (8%)
    all_to_all x3, blocking collectives, exchanged(): return lax.all_to_all(value, axes, split_axis=0, concat_axis=0, tiled=True)  82.5 us
    ppermute x10, starting transfers between devices, moved(): lax.ppermute(value, AX, [(i, (i + step) % size) for i in range(size)])  16.4 us
    ppermute x10, waiting for transfers between devices, moved(): lax.ppermute(value, AX, [(i, (i + step) % size) for i in range(size)])  12.2 us
    pallas_call x1, Pallas kernels, way_up(): call(up_kernel, (shaped(own.shape, F32, False), shaped((slots, ROWS, 128)...  11.7 us
    pallas_call x1, Pallas kernels, build(): call(build_kernel, shaped((slots, ROWS, 128), BF16), [SMEM, SMEM, VMEM, V...  8.48 us
    pallas_call x1, Pallas kernels, place(): call(place_kernel, (shaped(fluid.shape, F32), shaped((5, 64, 128), F32),...  7.44 us
    pallas_call x1, Pallas kernels, read(): call(read_kernel, shaped(positions.shape, F32, False), [SMEM, VMEM, VMEM]...  6.15 us
  transfers between devices with their start and end apart: 10, of which 3 were waited for; matrix products, arithmetic and copies ran while one was open for 0% of the time, Pallas kernels for 0%

profile of v5, /device:TPU:1, one launch (start us, length us, event | category | flops | bytes accessed | tf_op | source)
XLA Modules:
  0.0 148.7 jit_solution(3525708967092739835)
XLA Ops:
  0.6 8.5 %shard_map.68 = bf16[128,48,128]{2,1,0:T(8,128)(2,1)S(1)} custom-call(s32[1,128]{1,0:T(1,128)} %bitcast.10, s32[2,128]{1,0:T(2,128)} %bitcast.12, f32[3,128,256]{2,1,0:T(8,128)} %bitcast.6, f32[3,128,256]{2,1,0:T(8,128)} %bitcast.8, f32[4,3,128,128]{3,2,1,0:T(8,128)} %fluid_ref.3), custom_call_target="tpu_custom_call" | custom-call | tf_op jit(solution)/shard_map/pallas_call | solution.py:223
  9.1 0.0 copy-start
  9.1 36.1 %all_to_all.15.pay_ref = bf16[128,48,128]{2,1,0:T(8,128)(2,1)S(1)} all-to-all(bf16[128,48,128]{2,1,0:T(8,128)(2,1)S(1)} %shard_map.68), channel_id=1, replica_groups=mesh['hi'=16,'lo'=8] {'hi','lo'}, dimensions={0} | all-to-all | bytes 3145728 | tf_op jit(solution)/shard_map/all_to_all | solution.py:755
  45.3 1.1 slice.3
  46.4 0.2 convert_reduce_fusion
  46.6 0.1 reshape.16.meta_ref
  46.7 0.0 copy-done
  46.7 7.4 %shard_map.69 = (f32[4,3,128,128]{3,2,1,0:T(8,128)S(1)}, f32[5,64,128]{2,1,0:T(8,128)S(1)}, f32[5,64,128]{2,1,0:T(8,128)S(1)}, bf16[2,64,128]{2,1,0:T(8,128)(2,1...) custom-call(s32[1024]{0:T(1024)S(1)} %reshape.16.meta_ref, bf16[128,48,128]{2,1,0:T(8,128)(2,1)S(1)} %all_to_all.15.pay_ref, ...), custom_call_target="tpu_custom_call" | custom-call | tf_op jit(solution)/shard_map/pallas_call | solution.py:393
  54.1 1.2 collective-permute-start
  55.3 0.0 collective-permute-start.1
  55.4 0.2 collective-permute-start.2
  55.5 6.7 %collective-permute-start.3 = (bf16[2,64,128]{2,1,0:T(8,128)(2,1)S(1)}, bf16[2,64,128]{2,1,0:T(8,128)(2,1)S(1)}, u32[]{:S(2)}, u32[]{:S(2)}) collective-permute-start(bf16[2,64,128]{2,1,0:T(8,128)(2,1)S(1)} %get-tuple-element.19), channel_id=1, source_target_pairs={{0,126},{1,127},{2,0},{3,1},{4,2},{5,3},{6,4},{7,5},{8,6},{9,7},{1... | collective-permute-start | bytes 98312 | tf_op jit(solution)/shard_map/ppermute | solution.py:751
  62.2 2.8 %collective-permute-done.2.m2_ref = bf16[2,64,128]{2,1,0:T(8,128)(2,1)S(1)} collective-permute-done((bf16[2,64,128]{2,1,0:T(8,128)(2,1)S(1)}, bf16[2,64,128]{2,1,0:T(8,128)(2,1)S(1)}, u32[]{:S(2)}, u32[]{:S(2)}) %collective-permute-start.2) | collective-permute-done | bytes 32800 | tf_op jit(solution)/shard_map/ppermute | solution.py:751
  65.0 0.0 collective-permute-done.3.p2_ref
  65.0 0.0 collective-permute-done.m1_ref
  65.0 0.0 collective-permute-done.1.p1_ref
  65.0 1.7 %shard_map.70 = (f32[3,3,64,128]{3,2,1,0:T(8,128)S(1)}, f32[8,24,128]{2,1,0:T(8,128)S(1)}, bf16[1728,128]{1,0:T(8,128)(2,1)}, bf16[1728,128]{1,0:T(8,128)(2,1)S(1)}) custom-call(f32[4,3,128,128]{3,2,1,0:T(8,128)S(1)} %get-tuple-element.15.src_ref.own_ref, f32[5,64,128]{2,1,0:T(8,128)S(1)} %get-tuple-element.16.up_ref, ...), custom_call_target="tpu_custom_call" | custom-call | tf_op jit(solution)/shard_map/pallas_call | solution.py:488
  66.7 0.9 collective-permute-start.8
  67.6 5.8 %collective-permute-start.9 = (bf16[1728,128]{1,0:T(8,128)(2,1)S(1)}, bf16[1728,128]{1,0:T(8,128)(2,1)S(1)}, u32[]{:S(2)}, u32[]{:S(2)}) collective-permute-start(bf16[1728,128]{1,0:T(8,128)(2,1)S(1)} %get-tuple-element.23), channel_id=1, source_target_pairs={{0,127},{1,0},{2,1},{3,2},{4,3},{5,4},{6,5},{7,6},{8,7},{9,8},{10,... | collective-permute-start | bytes 1327112 | tf_op jit(solution)/shard_map/ppermute | solution.py:751
  73.4 14.5 %all_to_all.16.g2_ref = f32[8,24,128]{2,1,0:T(8,128)S(1)} all-to-all(f32[8,24,128]{2,1,0:T(8,128)S(1)} %get-tuple-element.20), channel_id=1, replica_groups=mesh['hi'=16,'lo'=8] {'lo'}, dimensions={0} | all-to-all | bytes 196608 | tf_op jit(solution)/shard_map/all_to_all | solution.py:755
  87.9 0.1 collective-permute-start.7
  88.0 1.1 collective-permute-start.6
  89.1 0.5 collective-permute-start.5
  89.6 2.9 %collective-permute-done.7.g4_ref = bf16[8,24,128]{2,1,0:T(8,128)(2,1)S(1)} collective-permute-done((bf16[8,24,128]{2,1,0:T(8,128)(2,1)S(1)}, bf16[8,24,128]{2,1,0:T(8,128)(2,1)S(1)}, u32[]{:S(2)}, u32[]{:S(2)}) %collective-permute-start.7) | collective-permute-done | bytes 49184 | tf_op jit(solution)/shard_map/ppermute | solution.py:751
  92.4 0.0 collective-permute-start.4
  92.4 6.6 %collective-permute-done.4.g0_ref = bf16[8,24,128]{2,1,0:T(8,128)(2,1)S(1)} collective-permute-done((bf16[8,24,128]{2,1,0:T(8,128)(2,1)S(1)}, bf16[8,24,128]{2,1,0:T(8,128)(2,1)S(1)}, u32[]{:S(2)}, u32[]{:S(2)}) %collective-permute-start.4) | collective-permute-done | bytes 49184 | tf_op jit(solution)/shard_map/ppermute | solution.py:751
  99.0 0.0 collective-permute-done.6.g3_ref
  99.0 0.0 collective-permute-done.5.g1_ref
  99.0 0.0 collective-permute-done.8.low_ref
  99.0 0.0 collective-permute-done.9.high_ref
  99.0 11.7 %shard_map.71 = (f32[4,3,128,128]{3,2,1,0:T(8,128)}, bf16[128,48,128]{2,1,0:T(8,128)(2,1)S(1)}) custom-call(s32[1]{0:T(128)} %bitcast.me_ref, s32[1024]{0:T(1024)S(1)} %reshape.16.meta_ref, f32[8,128]{1,0:T(8,128)S(1)} %get-tuple-element.14.lift_ref, bf16[8,24,128]{2,1,0:T(8,128)(2,1)S(1)} %collective-permute-done.4.g0_ref, ...), custom_call_target="tpu_custom_call" | custom-call | tf_op jit(solution)/shard_map/pallas_call | solution.py:666
  110.7 0.0 copy-start.1
  110.7 31.8 %all_to_all.17.pay_ref = bf16[128,48,128]{2,1,0:T(8,128)(2,1)S(1)} all-to-all(bf16[128,48,128]{2,1,0:T(8,128)(2,1)S(1)} %get-tuple-element.25), channel_id=1, replica_groups=mesh['hi'=16,'lo'=8] {'hi','lo'}, dimensions={0} | all-to-all | bytes 3145728 | tf_op jit(solution)/shard_map/all_to_all | solution.py:755
  142.5 0.0 copy-done.1
  142.5 6.2 %shard_map.72 = f32[3,128,256]{2,1,0:T(8,128)} custom-call(s32[1,128]{1,0:T(1,128)} %bitcast.11, bf16[128,48,128]{2,1,0:T(8,128)(2,1)S(1)} %all_to_all.17.pay_ref, f32[3,128,256]{2,1,0:T(8,128)S(1)} %bitcast.7), custom_call_target="tpu_custom_call" | custom-call | tf_op jit(solution)/shard_map/pallas_call | solution.py:737
  (1 shorter events, 0.0 us)
Async XLA Ops:
  9.1 37.6 %copy-start = (f32[4,3,128,128]{3,2,1,0:T(8,128)S(1)}, f32[4,3,128,128]{3,2,1,0:T(8,128)}, u32[]{:S(2)}) copy-start(f32[4,3,128,128]{3,2,1,0:T(8,128)} %fluid_ref.3) | copy-start | bytes 2359300
  54.1 10.9 %collective-permute-start = (f32[5,64,128]{2,1,0:T(8,128)S(1)}, f32[5,64,128]{2,1,0:T(8,128)S(1)}, u32[]{:S(2)}, u32[]{:S(2)}) collective-permute-start(f32[5,64,128]{2,1,0:T(8,128)S(1)} %get-tuple-element.16.up_ref), channel_id=1, source_target_pairs={{0,1},{1,2},{2,3},{3,4},{4,5},{5,6},{6,7},{7,8},{8,9},{9,10},{10,1... | collective-permute-start | bytes 491528 | tf_op jit(solution)/shard_map/ppermute | solution.py:751
  55.3 9.7 %collective-permute-start.1 = (f32[5,64,128]{2,1,0:T(8,128)S(1)}, f32[5,64,128]{2,1,0:T(8,128)S(1)}, u32[]{:S(2)}, u32[]{:S(2)}) collective-permute-start(f32[5,64,128]{2,1,0:T(8,128)S(1)} %get-tuple-element.17.down_ref), channel_id=1, source_target_pairs={{0,127},{1,0},{2,1},{3,2},{4,3},{5,4},{6,5},{7,6},{8,7},{9,8},{10,... | collective-permute-start | bytes 491528 | tf_op jit(solution)/shard_map/ppermute | solution.py:751
  55.4 9.6 %collective-permute-start.2 = (bf16[2,64,128]{2,1,0:T(8,128)(2,1)S(1)}, bf16[2,64,128]{2,1,0:T(8,128)(2,1)S(1)}, u32[]{:S(2)}, u32[]{:S(2)}) collective-permute-start(bf16[2,64,128]{2,1,0:T(8,128)(2,1)S(1)} %get-tuple-element.18), channel_id=1, source_target_pairs={{0,2},{1,3},{2,4},{3,5},{4,6},{5,7},{6,8},{7,9},{8,10},{9,11},{10,... | collective-permute-start | bytes 98312 | tf_op jit(solution)/shard_map/ppermute | solution.py:751
  55.5 9.5 %collective-permute-start.3 = (bf16[2,64,128]{2,1,0:T(8,128)(2,1)S(1)}, bf16[2,64,128]{2,1,0:T(8,128)(2,1)S(1)}, u32[]{:S(2)}, u32[]{:S(2)}) collective-permute-start(bf16[2,64,128]{2,1,0:T(8,128)(2,1)S(1)} %get-tuple-element.19), channel_id=1, source_target_pairs={{0,126},{1,127},{2,0},{3,1},{4,2},{5,3},{6,4},{7,5},{8,6},{9,7},{1... | collective-permute-start | bytes 98312 | tf_op jit(solution)/shard_map/ppermute | solution.py:751
  66.7 32.3 %collective-permute-start.8 = (bf16[1728,128]{1,0:T(8,128)(2,1)}, bf16[1728,128]{1,0:T(8,128)(2,1)S(1)}, u32[]{:S(2)}, u32[]{:S(2)}) collective-permute-start(bf16[1728,128]{1,0:T(8,128)(2,1)} %get-tuple-element.22), channel_id=1, source_target_pairs={{0,1},{1,2},{2,3},{3,4},{4,5},{5,6},{6,7},{7,8},{8,9},{9,10},{10,1... | collective-permute-start | bytes 1327112 | tf_op jit(solution)/shard_map/ppermute | solution.py:751
  67.6 31.4 %collective-permute-start.9 = (bf16[1728,128]{1,0:T(8,128)(2,1)S(1)}, bf16[1728,128]{1,0:T(8,128)(2,1)S(1)}, u32[]{:S(2)}, u32[]{:S(2)}) collective-permute-start(bf16[1728,128]{1,0:T(8,128)(2,1)S(1)} %get-tuple-element.23), channel_id=1, source_target_pairs={{0,127},{1,0},{2,1},{3,2},{4,3},{5,4},{6,5},{7,6},{8,7},{9,8},{10,... | collective-permute-start | bytes 1327112 | tf_op jit(solution)/shard_map/ppermute | solution.py:751
  87.9 4.5 %collective-permute-start.7 = (bf16[8,24,128]{2,1,0:T(8,128)(2,1)S(1)}, bf16[8,24,128]{2,1,0:T(8,128)(2,1)S(1)}, u32[]{:S(2)}, u32[]{:S(2)}) collective-permute-start(bf16[8,24,128]{2,1,0:T(8,128)(2,1)S(1)} %convert_element_type.4), channel_id=1, source_target_pairs={{0,112},{1,113},{2,114},{3,115},{4,116},{5,117},{6,118},{7,119},{8... | collective-permute-start | bytes 147464 | tf_op jit(solution)/shard_map/ppermute | solution.py:751
  88.0 11.0 %collective-permute-start.6 = (f32[8,24,128]{2,1,0:T(8,128)S(1)}, f32[8,24,128]{2,1,0:T(8,128)S(1)}, u32[]{:S(2)}, u32[]{:S(2)}) collective-permute-start(f32[8,24,128]{2,1,0:T(8,128)S(1)} %all_to_all.16.g2_ref), channel_id=1, source_target_pairs={{0,120},{1,121},{2,122},{3,123},{4,124},{5,125},{6,126},{7,127},{8... | collective-permute-start | bytes 294920 | tf_op jit(solution)/shard_map/ppermute | solution.py:751
  89.1 9.9 %collective-permute-start.5 = (f32[8,24,128]{2,1,0:T(8,128)S(1)}, f32[8,24,128]{2,1,0:T(8,128)S(1)}, u32[]{:S(2)}, u32[]{:S(2)}) collective-permute-start(f32[8,24,128]{2,1,0:T(8,128)S(1)} %all_to_all.16.g2_ref), channel_id=1, source_target_pairs={{0,8},{1,9},{2,10},{3,11},{4,12},{5,13},{6,14},{7,15},{8,16},{9,17... | collective-permute-start | bytes 294920 | tf_op jit(solution)/shard_map/ppermute | solution.py:751
  92.4 6.6 %collective-permute-start.4 = (bf16[8,24,128]{2,1,0:T(8,128)(2,1)S(1)}, bf16[8,24,128]{2,1,0:T(8,128)(2,1)S(1)}, u32[]{:S(2)}, u32[]{:S(2)}) collective-permute-start(bf16[8,24,128]{2,1,0:T(8,128)(2,1)S(1)} %convert_element_type.4), channel_id=1, source_target_pairs={{0,16},{1,17},{2,18},{3,19},{4,20},{5,21},{6,22},{7,23},{8,24},{9,... | collective-permute-start | bytes 147464 | tf_op jit(solution)/shard_map/ppermute | solution.py:751
  110.7 31.8 %copy-start.1 = (f32[128,3,256]{2,0,1:T(8,128)S(1)}, f32[128,3,256]{2,0,1:T(8,128)}, u32[]{:S(2)}) copy-start(f32[128,3,256]{2,0,1:T(8,128)} %param.5) | copy-start | bytes 1179652
